TPU v7x, 1024 devices: a whole 4x4x32 slice. The times are simulated.
1024 devices in a mesh: ta: 4 (over x), gz: 64 (over y, z_lo, core), gy: 4 (over z_hi).
Axes of the slice: x: 4, y: 4, z: 32 (z_hi: 4, z_lo: 8; z = z_hi * 8 + z_lo), core: 2. Of those that a mesh axis runs over, the one named last changes fastest.
Arguments:
- propagator: bfloat16 [2, 4, 3, 12, 4, 64, 512], P(None, None, None, None, 'ta', 'gz', 'gy'), may hold values from -6 to 6
- links: bfloat16 [2, 3, 3, 4, 64, 512], P(None, None, None, 'ta', 'gz', 'gy'), may hold values from -2.5 to 2.5
- source_z: int32 [4, 4], replicated, may hold values from 0 to 63
- displacements: int32 [9], replicated, may hold values from 0 to 8, each once
- momenta: int32 [4], replicated, may hold values from 1 to 3
- gamma_perm: int32 [4, 4], replicated, may hold values from 0 to 3, each once within a row
- gamma_phase: int32 [4, 4], replicated, may hold values from 0 to 3
Outputs:
- correlator: float32 [4, 9, 4, 4, 2], replicated
Inputs may be any that keep to these rules, and one draw needn't show every extreme that they name: `displacements`: every displacement from -4 to 4 appears exactly once. `gamma_perm`: each row is a permutation of the four spin indices.
All inputs are finite; a program needn't handle non-finite values.
Results may differ from a plain program's by a relative error of at most 0.0003.
Values may be sent and summed in bfloat16 or wider, within the bound.
A program may use at most 32 MiB of HBM per device.

v0:
```python
import math

import jax
import jax.numpy as jnp
from jax import lax
from jax.sharding import Mesh
from jax.sharding import PartitionSpec as P

GZ = ("gz_0", "gz_1", "gz_2")
TA_GZ_GY = ("ta", "gz_0", "gz_1", "gz_2", "gy")


highest = lax.Precision.HIGHEST


def over_axes(array, axes):
    for axis in axes:
        array = lax.psum(array, axis)
    return array


def colour_apply(wilson, field_now):
    left_real = wilson[0][None, :, :, None, :]
    left_imag = wilson[1][None, :, :, None, :]
    right_real = field_now[0][:, None, :, :, :]
    right_imag = field_now[1][:, None, :, :, :]
    real_part = jnp.sum(left_real * right_real - left_imag * right_imag, axis=2)
    imag_part = jnp.sum(left_real * right_imag + left_imag * right_real, axis=2)
    return jnp.stack([real_part, imag_part])


def link_product(left_link, right_link):
    left_real = left_link[0][:, :, None, :]
    left_imag = left_link[1][:, :, None, :]
    right_real = right_link[0][None, :, :, :]
    right_imag = right_link[1][None, :, :, :]
    real_part = jnp.sum(left_real * right_real - left_imag * right_imag, axis=1)
    imag_part = jnp.sum(left_real * right_imag + left_imag * right_real, axis=1)
    return jnp.stack([real_part, imag_part])


def spin_pairs(source, field_now):
    source_real = source[0][:, None]
    source_imag = source[1][:, None]
    field_real = field_now[0][None]
    field_imag = field_now[1][None]
    real_part = jnp.sum(source_real * field_real + source_imag * field_imag, axis=(2, 3))
    imag_part = jnp.sum(source_real * field_imag - source_imag * field_real, axis=(2, 3))
    return (real_part, imag_part)


def site_traces(gamma_real, gamma_imag, pairs):
    pair_real, pair_imag = pairs
    table_real = gamma_real[:, :, :, None]
    table_imag = gamma_imag[:, :, :, None]
    real_part = jnp.sum(table_real * pair_real[None] - table_imag * pair_imag[None], axis=(1, 2))
    imag_part = jnp.sum(table_real * pair_imag[None] + table_imag * pair_real[None], axis=(1, 2))
    return (real_part, imag_part)


def gamma_tables(gamma_perm, gamma_phase):
    columns = jnp.arange(4, dtype=jnp.int32)
    hits = (gamma_perm[:, :, None] == columns[None, None, :]).astype(jnp.float32)
    real_part = (gamma_phase == 0).astype(jnp.float32) - (gamma_phase == 2).astype(jnp.float32)
    imag_part = (gamma_phase == 1).astype(jnp.float32) - (gamma_phase == 3).astype(jnp.float32)
    return (hits * real_part[:, :, None], hits * imag_part[:, :, None])


def body(propagator, links, source_z, displacements, momenta, gamma_perm, gamma_phase):
    gamma_real, gamma_imag = gamma_tables(gamma_perm, gamma_phase)
    adjoint_real = jnp.swapaxes(gamma_real, 1, 2)
    adjoint_imag = -jnp.swapaxes(gamma_imag, 1, 2)
    depth_count = lax.axis_size(GZ)
    nsteps = (displacements.shape[0] - 1) // 2
    slices_dev = propagator.shape[4]
    sites_dev = propagator.shape[6]
    slices_all = slices_dev * lax.axis_size("ta")
    sites_total = sites_dev * lax.axis_size("gy") * depth_count
    scaling = 1.0 / (24.0 * math.sqrt(sites_total))
    field_data, link_data = (
        lax.all_to_all(propagator, GZ, split_axis=6, concat_axis=5, tiled=True),
        lax.all_to_all(links[:, :, :, None], GZ, split_axis=6, concat_axis=5, tiled=True),
    )
    link_data = link_data[:, :, :, 0]
    block_sites = field_data.shape[-1]
    line_length = depth_count * block_sites
    flat_length = slices_dev * line_length
    field_flat = jnp.reshape(field_data, (2, 4, 3, 12, flat_length))
    links_flat = jnp.reshape(link_data, (2, 3, 3, flat_length))

    def roll_lines(array, offset):
        shaped = jnp.reshape(array, array.shape[:-1] + (slices_dev, line_length))
        return jnp.reshape(jnp.roll(shaped, offset * block_sites, axis=-1), array.shape)

    positions = jnp.arange(flat_length, dtype=jnp.int32)
    depth_flat = positions // block_sites % depth_count
    slice_flat = lax.axis_index("ta") * slices_dev + positions // line_length
    slice_ids = jnp.arange(slices_all, dtype=jnp.int32)
    slice_hits = slice_ids[:, None] == slice_flat[None, :]
    source_flat = jnp.sum(jnp.where(slice_hits[:, None, :], source_z[:, :, None], 0), axis=0)
    turn_count = momenta[:, None] * (depth_flat[None, :] - source_flat) % depth_count
    angles = turn_count.astype(jnp.float32) * (2.0 * math.pi / depth_count)
    cosine = jnp.cos(angles)
    sine_table = jnp.sin(angles)
    slice_weight = slice_hits.astype(jnp.float32)

    def contract(trace, table):
        return jnp.einsum("tl,gl,pl->tgp", slice_weight, trace, table, precision=highest)

    def project(traces):
        trace_real, trace_imag = traces
        real_part = contract(trace_real, cosine) + contract(trace_imag, sine_table)
        imag_part = contract(trace_imag, cosine) - contract(trace_real, sine_table)
        return jnp.stack([real_part, imag_part], axis=-1) * scaling

    source = field_flat.astype(jnp.float32)
    unit = jnp.broadcast_to(jnp.eye(3, dtype=jnp.float32)[:, :, None], (3, 3, flat_length))
    identity = jnp.stack([unit, jnp.zeros_like(unit)])
    results = {0: project(site_traces(gamma_real, gamma_imag, spin_pairs(source, source)))}
    wilson = identity
    moved_field = field_flat
    moved_links = links_flat
    for reach in range(1, nsteps + 1):
        wilson = link_product(wilson, moved_links.astype(jnp.float32))
        moved_field, moved_links = (roll_lines(moved_field, -1), roll_lines(moved_links, -1))
        pairs = spin_pairs(source, colour_apply(wilson, moved_field.astype(jnp.float32)))
        results[reach] = project(site_traces(gamma_real, gamma_imag, pairs))
        mirrored_trace_real, mirrored_trace_imag = site_traces(adjoint_real, adjoint_imag, pairs)
        other_real = contract(mirrored_trace_real, cosine) - contract(
            mirrored_trace_imag, sine_table
        )
        other_imag = contract(mirrored_trace_imag, cosine) + contract(
            mirrored_trace_real, sine_table
        )
        shift_turn = momenta * reach % depth_count
        shift_angle = shift_turn.astype(jnp.float32) * (2.0 * math.pi / depth_count)
        shift_cos = jnp.cos(shift_angle)
        shift_sin = jnp.sin(shift_angle)
        mirrored_real_part = other_real * shift_cos - other_imag * shift_sin
        mirrored_imag_part = -other_imag * shift_cos - other_real * shift_sin
        results[-reach] = jnp.stack([mirrored_real_part, mirrored_imag_part], axis=-1) * scaling
    stacked = jnp.stack([results[offset] for offset in range(-nsteps, nsteps + 1)], axis=1)
    offsets = jnp.arange(2 * nsteps + 1, dtype=jnp.int32)
    select = (displacements[:, None] == offsets[None, :]).astype(jnp.float32)
    ordered = jnp.einsum("jl,tlgpc->tjgpc", select, stacked, precision=highest)
    return over_axes(ordered, TA_GZ_GY)


def solution(mesh):
    torus = Mesh(
        mesh.devices.reshape(mesh.shape["ta"], 4, 8, 2, mesh.shape["gy"]),
        ("ta", "gz_0", "gz_1", "gz_2", "gy"),
    )
    in_specs = (
        P(None, None, None, None, "ta", GZ, "gy"),
        P(None, None, None, "ta", GZ, "gy"),
        P(),
        P(),
        P(),
        P(),
        P(),
    )
    out_specs = P()
    return jax.shard_map(body, mesh=torus, in_specs=in_specs, out_specs=out_specs, check_vma=False)
```

profile of v0, /device:TPU:1, one launch (start us, length us, event | category | flops | bytes accessed | tf_op | source)
XLA Modules:
  0.0 207.8 jit_solution(9183982287120262442)
XLA Ops:
  0.0 1.5 copy.270
  1.5 18.2 %all-to-all-start.1 = ((bf16[2,3,3,1,1,1,128]{2,0,5,4,3,1,6:T(2,128)(2,1)}), bf16[2,3,3,1,1,1,128]{2,0,5,4,3,1,6:T(2,128)(2,1)S(1)}, u32[]{:S(2)}, u32[]{:S(2)}) async-start(bf16[2,3,3,1,1,1,128]{2,0,5,4,3,1,6:T(2,128)(2,1)} %bitcast.2), calls=%async_computation.1 | async-start | bytes 393216 | tf_op jit(solution)/shard_map/all_to_all | solution.py:82
  19.7 0.7 convert_subtract_fusion.1
  20.4 1.3 fusion.232
  21.7 0.8 select_reduce_fusion
  22.5 0.8 fusion.240
  23.3 1.4 fusion.102
  24.7 1.4 copy.267
  26.2 1.6 reshape.469
  27.8 0.6 sin.19
  28.4 0.5 sin.18
  28.9 0.6 sin.17
  29.5 0.6 sin.16
  30.1 6.3 %all-to-all-done.1 = bf16[2,3,3,1,1,1,128]{2,0,5,4,3,1,6:T(2,128)(2,1)S(1)} async-done(((bf16[2,3,3,1,1,1,128]{2,0,5,4,3,1,6:T(2,128)(2,1)}), bf16[2,3,3,1,1,1,128]{2,0,5,4,3,1,6:T(2,128)(2,1)S(1)}, u32[]{:S(2)}, u32[]{:S(2)}) %all-to-all-start.1) | async-done | bytes 4640 | tf_op jit(solution)/shard_map/all_to_all | solution.py:82
  36.4 6.9 %all-to-all-start = ((bf16[64,2,288]{2,1,0:T(2,128)(2,1)}), bf16[64,2,288]{2,1,0:T(2,128)(2,1)S(1)}, u32[]{:S(2)}, u32[]{:S(2)}) async-start(bf16[64,2,288]{2,1,0:T(2,128)(2,1)} %reshape.469), calls=%async_computation | async-start | bytes 196608 | tf_op jit(solution)/shard_map/all_to_all | solution.py:81
  44.8 0.6 subtract_reduce_fusion.18
  45.5 11.4 %all-to-all-done = bf16[64,2,288]{2,1,0:T(2,128)(2,1)S(1)} async-done(((bf16[64,2,288]{2,1,0:T(2,128)(2,1)}), bf16[64,2,288]{2,1,0:T(2,128)(2,1)S(1)}, u32[]{:S(2)}, u32[]{:S(2)}) %all-to-all-start) | async-done | bytes 73760 | tf_op jit(solution)/shard_map/all_to_all | solution.py:81
  56.8 0.7 reshape.470
  57.5 0.7 copy.276
  59.0 1.2 fusion.242
  60.8 0.7 slice_bitcast_fusion.5
  61.5 0.6 slice_bitcast_fusion.3
  62.2 0.9 copy.268
  63.1 0.9 copy.277
  64.1 0.3 slice_bitcast_fusion.11
  64.4 0.3 copy.269
  64.8 0.3 copy.278
  66.1 1.0 add_reduce_fusion
  67.1 0.4 subtract_reduce_fusion.9
  68.0 0.2 copy.313
  68.4 0.2 copy.314
  69.4 0.2 copy.310
  70.2 0.2 copy.305
  70.5 0.2 copy.306
  71.2 0.2 copy.301
  71.6 0.2 copy.302
  72.3 0.2 copy.297
  73.6 0.2 copy.293
  74.7 0.2 copy.289
  75.8 0.2 copy.285
  77.6 0.4 stack.128
  78.0 0.2 convolution_bitcast_fusion
  78.3 12.7 %psum.35 = f32[4,9,4,4,2]{1,3,4,2,0:T(4,128)S(1)} all-reduce(f32[4,9,4,4,2]{1,3,4,2,0:T(4,128)S(1)} %convolution_bitcast_fusion), channel_id=1, replica_groups=mesh['ta'=4,'gz_0'=4,'gz_1'=8,'gz_2'=2,'gy'=4] {'ta'}, use_global_device_ids=true, to_apply=%region_45.46 | all-reduce | flops 1152 | bytes 9216 | tf_op jit(solution)/shard_map/psum | solution.py:18
  91.0 11.9 %psum.36 = f32[4,9,4,4,2]{1,3,4,2,0:T(4,128)S(1)} all-reduce(f32[4,9,4,4,2]{1,3,4,2,0:T(4,128)S(1)} %psum.35), channel_id=1, replica_groups=mesh['ta'=4,'gz_0'=4,'gz_1'=8,'gz_2'=2,'gy'=4] {'gz_0'}, use_global_device_ids=true, to_apply=%region_46.47 | all-reduce | flops 1152 | bytes 9216 | tf_op jit(solution)/shard_map/psum | solution.py:18
  102.9 44.9 %psum.37 = f32[4,9,4,4,2]{1,3,4,2,0:T(4,128)S(1)} all-reduce(f32[4,9,4,4,2]{1,3,4,2,0:T(4,128)S(1)} %psum.36), channel_id=1, replica_groups=mesh['ta'=4,'gz_0'=4,'gz_1'=8,'gz_2'=2,'gy'=4] {'gz_1'}, use_global_device_ids=true, to_apply=%region_47.48 | all-reduce | flops 1152 | bytes 9216 | tf_op jit(solution)/shard_map/psum | solution.py:18
  147.9 18.4 %psum.38 = f32[4,9,4,4,2]{1,3,4,2,0:T(4,128)S(1)} all-reduce(f32[4,9,4,4,2]{1,3,4,2,0:T(4,128)S(1)} %psum.37), channel_id=1, replica_groups=mesh['ta'=4,'gz_0'=4,'gz_1'=8,'gz_2'=2,'gy'=4] {'gz_2'}, use_global_device_ids=true, to_apply=%region_48.49 | all-reduce | flops 1152 | bytes 9216 | tf_op jit(solution)/shard_map/psum | solution.py:18
  166.2 40.9 %psum.39 = f32[4,9,4,4,2]{1,3,4,2,0:T(4,128)S(1)} all-reduce(f32[4,9,4,4,2]{1,3,4,2,0:T(4,128)S(1)} %psum.38), channel_id=1, replica_groups=mesh['ta'=4,'gz_0'=4,'gz_1'=8,'gz_2'=2,'gy'=4] {'gy'}, use_global_device_ids=true, to_apply=%region_49.50 | all-reduce | flops 1152 | bytes 9216 | tf_op jit(solution)/shard_map/psum | solution.py:18
  207.1 0.7 copy.315
  (147 shorter events, 11.4 us)
Async XLA Ops:
  1.5 34.8 %all-to-all-start.1 = ((bf16[2,3,3,1,1,1,128]{2,0,5,4,3,1,6:T(2,128)(2,1)}), bf16[2,3,3,1,1,1,128]{2,0,5,4,3,1,6:T(2,128)(2,1)S(1)}, u32[]{:S(2)}, u32[]{:S(2)}) async-start(bf16[2,3,3,1,1,1,128]{2,0,5,4,3,1,6:T(2,128)(2,1)} %bitcast.2), calls=%async_computation.1 | async-start | bytes 393216 | tf_op jit(solution)/shard_map/all_to_all | solution.py:82
  36.4 20.5 %all-to-all-start = ((bf16[64,2,288]{2,1,0:T(2,128)(2,1)}), bf16[64,2,288]{2,1,0:T(2,128)(2,1)S(1)}, u32[]{:S(2)}, u32[]{:S(2)}) async-start(bf16[64,2,288]{2,1,0:T(2,128)(2,1)} %reshape.469), calls=%async_computation | async-start | bytes 196608 | tf_op jit(solution)/shard_map/all_to_all | solution.py:81
  44.7 14.3 %copy-start.6 = (f32[3,3,128]{2,1,0:T(4,128)}, f32[3,3,128]{2,1,0:T(4,128)S(1)}, u32[]{:S(2)}) copy-start(f32[3,3,128]{2,1,0:T(4,128)S(1)} %get-tuple-element.54) | copy-start | bytes 13828
  44.7 14.3 %copy-start.8 = (f32[3,3,128]{2,1,0:T(4,128)}, f32[3,3,128]{2,1,0:T(4,128)S(1)}, u32[]{:S(2)}) copy-start(f32[3,3,128]{2,1,0:T(4,128)S(1)} %get-tuple-element.51) | copy-start | bytes 13828
  44.7 14.3 %copy-start.10 = (f32[3,3,128]{2,1,0:T(4,128)}, f32[3,3,128]{2,1,0:T(4,128)S(1)}, u32[]{:S(2)}) copy-start(f32[3,3,128]{2,1,0:T(4,128)S(1)} %get-tuple-element.52) | copy-start | bytes 13828
  60.4 1.7 copy-start
  64.3 0.9 copy-start.2
  64.3 0.9 copy-start.3
  64.3 0.9 copy-start.9
  64.4 0.9 copy-start.11
  64.4 1.1 copy-start.1
  64.4 1.1 copy-start.7
  64.4 1.5 copy-start.16
  64.4 1.5 copy-start.17
  64.4 1.7 copy-start.4
  64.4 1.7 copy-start.5
  64.7 2.4 %copy-start.12 = (f32[4,4,4]{2,1,0:T(4,128)S(1)}, f32[4,4,4]{2,1,0:T(4,128)}, u32[]{:S(2)}) copy-start(f32[4,4,4]{2,1,0:T(4,128)} %get-tuple-element.120) | copy-start | bytes 772
  64.7 2.4 %copy-start.13 = (f32[4,4,4]{2,1,0:T(4,128)S(1)}, f32[4,4,4]{2,1,0:T(4,128)}, u32[]{:S(2)}) copy-start(f32[4,4,4]{2,1,0:T(4,128)} %get-tuple-element.121) | copy-start | bytes 772
  64.7 2.4 %copy-start.14 = (f32[4,4,4]{2,1,0:T(4,128)S(1)}, f32[4,4,4]{2,1,0:T(4,128)}, u32[]{:S(2)}) copy-start(f32[4,4,4]{2,1,0:T(4,128)} %get-tuple-element.124) | copy-start | bytes 772
  64.7 2.4 %copy-start.15 = (f32[4,4,4]{2,1,0:T(4,128)S(1)}, f32[4,4,4]{2,1,0:T(4,128)}, u32[]{:S(2)}) copy-start(f32[4,4,4]{2,1,0:T(4,128)} %get-tuple-element.125) | copy-start | bytes 772
  65.4 8.0 %copy-start.20 = (f32[4]{0:T(128)S(1)}, f32[4]{0:T(128)}, u32[]{:S(2)}) copy-start(f32[4]{0:T(128)} %get-tuple-element.73) | copy-start | bytes 52
  65.4 8.0 %copy-start.25 = (f32[4]{0:T(128)S(1)}, f32[4]{0:T(128)}, u32[]{:S(2)}) copy-start(f32[4]{0:T(128)} %sin.19) | copy-start | bytes 52
  65.5 9.0 %copy-start.19 = (f32[4]{0:T(128)S(1)}, f32[4]{0:T(128)}, u32[]{:S(2)}) copy-start(f32[4]{0:T(128)} %get-tuple-element.132) | copy-start | bytes 52
  65.5 9.0 %copy-start.24 = (f32[4]{0:T(128)S(1)}, f32[4]{0:T(128)}, u32[]{:S(2)}) copy-start(f32[4]{0:T(128)} %sin.18) | copy-start | bytes 52
  65.7 9.9 %copy-start.18 = (f32[4]{0:T(128)S(1)}, f32[4]{0:T(128)}, u32[]{:S(2)}) copy-start(f32[4]{0:T(128)} %get-tuple-element.128) | copy-start | bytes 52
  65.7 9.9 %copy-start.23 = (f32[4]{0:T(128)S(1)}, f32[4]{0:T(128)}, u32[]{:S(2)}) copy-start(f32[4]{0:T(128)} %sin.17) | copy-start | bytes 52
  65.7 11.0 %copy-start.22 = (f32[4]{0:T(128)S(1)}, f32[4]{0:T(128)}, u32[]{:S(2)}) copy-start(f32[4]{0:T(128)} %sin.16) | copy-start | bytes 52
  69.3 8.8 %copy-start.21 = (s32[9]{0:T(128)S(1)}, s32[9]{0:T(128)}, u32[]{:S(2)}) copy-start(s32[9]{0:T(128)} %param.10) | copy-start | bytes 112
where the time goes:
time: 209 us; the launch traced here: 208 us
  blocking collectives  129 us (62%)
  starting transfers between devices  25.1 us (12%)
  local copies, waits for them, and re-layouts  19.8 us (9%)
  waiting for transfers between devices  17.6 us (8%)
  other arithmetic  9.52 us (5%)
  matrix products  6.11 us (3%)
    psum x5, blocking collectives, over_axes(): array = lax.psum(array, axis)  129 us
    all_to_all x1, starting transfers between devices, body(): lax.all_to_all(links[:, :, :, None], GZ, split_axis=6, concat_axis=5, til...  18.2 us
    all_to_all x1, waiting for transfers between devices, body(): lax.all_to_all(propagator, GZ, split_axis=6, concat_axis=5, tiled=True)  11.4 us
    all_to_all x1, starting transfers between devices, body(): lax.all_to_all(propagator, GZ, split_axis=6, concat_axis=5, tiled=True)  6.92 us
    all_to_all x1, waiting for transfers between devices, body(): lax.all_to_all(links[:, :, :, None], GZ, split_axis=6, concat_axis=5, til...  6.27 us
    dot_general x36, matrix products, contract(): jnp.einsum('tl,gl,pl->tgp', slice_weight, trace, table, precision=highest)  5.87 us
    unnamed x59, local copies, waits for them, and re-layouts  5.54 us
  transfers between devices with their start and end apart: 2, of which 2 were waited for; matrix products, arithmetic and copies ran while one was open for 6% of the time, Pallas kernels for 0%

commit v1 on v0

v1 whole, which is shorter than its diff:
```python
import functools
import math

import jax
import jax.numpy as jnp
from jax import lax
from jax.experimental import pallas as pl
from jax.experimental.pallas import tpu as pltpu
from jax.sharding import Mesh
from jax.sharding import PartitionSpec as P

GZ = ("gz_0", "gz_1", "gz_2")
MESH = pl.DeviceIdType.MESH
F32 = jnp.float32
I32 = jnp.int32


def roll4(x, r):
    if r == 0:
        return x
    spin = lax.broadcasted_iota(I32, (8, 128), 0) % 4
    return jnp.where(spin < 4 - r, pltpu.roll(x, 8 - r, 0), pltpu.roll(x, 4 - r, 0))


def kernel(
    nz, scaling, s_hbm, u_hbm, source_z, displacements, momenta, perm, phase, out,
    sbuf, ubuf, left, fields, wil, table, kind, mine, slot_a, sum_a, slot_b, sum_b, slot_c,
    load_sem, send_sem, recv_sem, ready, send_a, recv_a, send_b, recv_b, send_c, recv_c,
):
    x = lax.axis_index("ta")
    gy0 = lax.axis_index("gz_0")
    lo = lax.axis_index("gz_1")
    core = lax.axis_index("gz_2")
    hi = lax.axis_index("gy")
    z = gy0 * 16 + lo * 2 + core
    r = gy0 * 2 + core
    is_root = r == lo

    def along(offset):
        w = (z + (offset + nz)) % nz
        return {"gz_0": w // 16, "gz_1": (w // 2) % 8, "gz_2": w % 2}

    def replica(dx, dr):
        q = (r + dr) % 8
        return {"ta": (x + dx) % 4, "gz_0": q // 2, "gz_2": q % 2}

    load_s = pltpu.make_async_copy(s_hbm, sbuf.at[0], load_sem.at[0])
    load_u = pltpu.make_async_copy(u_hbm, ubuf.at[0], load_sem.at[1])
    load_s.start()
    load_u.start()

    barrier = pltpu.get_barrier_semaphore()
    for offset in (-2, -1, 1, 2):
        pl.semaphore_signal(barrier, inc=1, device_id=along(offset), device_id_type=MESH)

    @pl.loop(1, 32)
    def _(n):
        pl.semaphore_signal(barrier, inc=1, device_id=replica(n // 8, n % 8), device_id_type=MESH)

    lower = (hi + jnp.where(lo >= r, 0, 3)) % 4
    for step in (0, 1):
        seat = jnp.where(is_root, (hi + 3 + 2 * step) % 4, (lower + step) % 4)
        pl.semaphore_signal(barrier, inc=1, device_id={"gy": seat, "gz_1": r}, device_id_type=MESH)

    sub = lax.broadcasted_iota(I32, (8, 128), 0)
    lane = lax.broadcasted_iota(I32, (8, 128), 1)
    u_id = sub % 4
    g_id = (lane % 32) // 8
    p_id = (lane // 2) % 4
    c_id = lane % 2
    perm_t = jnp.zeros((8, 128), I32)
    phase_t = jnp.zeros((8, 128), I32)
    for g in range(4):
        for s in range(4):
            here = (g_id == g) & (u_id == s)
            perm_t = jnp.where(here, perm[g, s], perm_t)
            phase_t = jnp.where(here, phase[g, s], phase_t)
    mom = jnp.zeros((8, 128), I32)
    src = jnp.zeros((8, 128), I32)
    for p in range(4):
        mom = jnp.where(p_id == p, momenta[p], mom)
        src = jnp.where(p_id == p, source_z[x, p], src)
    for m in range(3):
        j_id = m * 4 + lane // 32
        shift = jnp.zeros((8, 128), I32)
        for j in range(4 * m, min(4 * m + 4, 9)):
            shift = jnp.where(j_id == j, displacements[j] - 4, shift)
        neg = shift < 0
        k_id = jnp.where(neg, -shift, shift)
        at = z - jnp.where(k_id >= 3, 2, 0) + jnp.where(neg, k_id, 0)
        turns = (mom * (at - src)) & (nz - 1)
        angle = turns.astype(F32) * (2.0 * math.pi / nz)
        cosine = jnp.cos(angle) * scaling
        sine = jnp.sin(angle) * scaling
        kind[m] = k_id
        for rr in range(4):
            s_id = (u_id + rr) % 4
            perm_r = pltpu.roll(perm_t, 8 - rr, 0) if rr else perm_t
            phase_r = pltpu.roll(phase_t, 8 - rr, 0) if rr else phase_t
            match = jnp.where(neg, perm_t, perm_r) == jnp.where(neg, s_id, u_id)
            power = jnp.where(neg, phase_t, phase_r)
            for ri in range(2):
                if ri == 0:
                    turn = jnp.where(c_id == 0, 0, 3)
                else:
                    turn = jnp.where(c_id == 0, jnp.where(neg, 3, 1), jnp.where(neg, 2, 0))
                h = (power + turn) & 3
                value = jnp.where((h & 1) == 1, sine, cosine)
                value = jnp.where(h >= 2, -value, value)
                table[m, rr * 2 + ri] = jnp.where(match & (j_id < 9), value, 0.0)

    load_s.wait()
    load_u.wait()

    @pl.loop(0, 18)
    def _(n):
        rows = sbuf[0, pl.ds(pl.multiple_of(n * 16, 16), 16), :].astype(F32)
        for half in range(2):
            for rr in range(4):
                left[rr, 2 * n + half] = roll4(rows[half * 8 : half * 8 + 8], rr)

    pl.semaphore_wait(barrier, 35 + jnp.where(is_root, 16, 0))

    def to(buf, n, dst, offset):
        return pltpu.make_async_remote_copy(
            src_ref=buf.at[0], dst_ref=buf.at[dst], send_sem=send_sem.at[n], recv_sem=recv_sem.at[n],
            device_id=along(offset), device_id_type=MESH,
        )

    halo = [
        to(sbuf, 0, 2, -2), to(sbuf, 1, 1, -1), to(sbuf, 2, 3, 2),
        to(ubuf, 3, 1, -1), to(ubuf, 4, 2, 1), to(ubuf, 5, 3, 2),
    ]
    for n in (3, 4, 5, 0, 1, 2):
        halo[n].start()

    @pl.when(is_root)
    def _():
        for step in (1, 3):
            pl.semaphore_signal(ready, inc=1, device_id={"gy": (hi + step) % 4}, device_id_type=MESH)

    def link(slot):
        block = ubuf[slot].astype(F32)
        return [
            [tuple(jnp.broadcast_to(block[3 * a + b, ri : ri + 1, :], (8, 128)) for ri in range(2)) for b in range(3)]
            for a in range(3)
        ]

    def product(one, two):
        def entry(a, c):
            re = im = None
            for b in range(3):
                (pr, pi), (qr, qi) = one[a][b], two[b][c]
                r2, i2 = pr * qr - pi * qi, pr * qi + pi * qr
                re, im = (r2, i2) if b == 0 else (re + r2, im + i2)
            return re, im

        return [[entry(a, c) for c in range(3)] for a in range(3)]

    for n in (3, 4, 5):
        halo[n].wait()
    base = link(0)
    ahead = product(base, link(1))
    back = product(link(3), link(2))
    for a in range(3):
        for b in range(3):
            for ri in range(2):
                wil[0, (a * 3 + b) * 2 + ri] = base[a][b][ri]
                wil[1, (a * 3 + b) * 2 + ri] = ahead[a][b][ri]
                wil[2, (a * 3 + b) * 2 + ri] = back[b][a][ri] if ri == 0 else -back[b][a][ri]

    def transport(slot, line):
        @pl.loop(0, 3)
        def _(q):
            got = [
                [sbuf[slot, pl.ds(pl.multiple_of((ri * 3 + b) * 48 + q * 16, 16), 16), :].astype(F32) for ri in range(2)]
                for b in range(3)
            ]
            for half in range(2):
                part = [[v[half * 8 : half * 8 + 8] for v in pair] for pair in got]
                for a in range(3):
                    re = im = None
                    for b in range(3):
                        wr, wi = wil[line, (a * 3 + b) * 2], wil[line, (a * 3 + b) * 2 + 1]
                        vr, vi = part[b]
                        r2, i2 = wr * vr - wi * vi, wr * vi + wi * vr
                        re, im = (r2, i2) if b == 0 else (re + r2, im + i2)
                    fields[line, a * 6 + q * 2 + half] = re
                    fields[line, 18 + a * 6 + q * 2 + half] = im

    halo[1].wait()
    transport(1, 0)
    halo[0].wait()
    transport(2, 1)
    halo[2].wait()
    transport(3, 2)

    kinds = [kind[m] for m in range(3)]
    total = [jnp.zeros((8, 128), F32) for _ in range(3)]
    for rr in range(4):
        def add(n, acc):
            acc = list(acc)
            for a in range(3):
                re_at, im_at = n + 6 * a, 18 + n + 6 * a
                sr, si = left[rr, re_at], left[rr, im_at]
                lr, li = roll4(fields[2, re_at], rr), roll4(fields[2, im_at], rr)
                right = [
                    (left[0, re_at], left[0, im_at]),
                    (fields[0, re_at], fields[0, im_at]),
                    (fields[1, re_at], fields[1, im_at]),
                ]
                for k, ((ar, ai), (br, bi)) in enumerate(
                    [((sr, si), right[0]), ((sr, si), right[1]), ((sr, si), right[2]), ((lr, li), right[1]), ((lr, li), right[2])]
                ):
                    acc[2 * k] = acc[2 * k] + (ar * br + ai * bi)
                    acc[2 * k + 1] = acc[2 * k + 1] + (ar * bi - ai * br)
            return tuple(acc)

        sums = lax.fori_loop(0, 6, add, tuple(jnp.zeros((8, 128), F32) for _ in range(10)))
        for ri in range(2):
            lines = [jnp.broadcast_to(jnp.sum(sums[2 * k + ri], axis=1, keepdims=True), (8, 128)) for k in range(5)]
            for m in range(3):
                value = lines[0]
                for k in range(1, 5):
                    value = jnp.where(kinds[m] == k, lines[k], value)
                total[m] = total[m] + table[m, rr * 2 + ri] * value
    flat = [jnp.sum(t, axis=0, keepdims=True) for t in total]
    flat.append(jnp.zeros((1, 128), F32))
    partial = jnp.concatenate(flat, axis=0)

    mine[...] = partial

    def to_root(slot):
        return pltpu.make_async_remote_copy(
            src_ref=mine, dst_ref=slot_a.at[slot], send_sem=send_a, recv_sem=recv_a.at[slot],
            device_id={"gz_0": lo // 2, "gz_2": lo % 2}, device_id_type=MESH,
        )

    def to_column(step):
        seat = (hi * 8 + lo + step) % 32
        return pltpu.make_async_remote_copy(
            src_ref=sum_a, dst_ref=slot_b.at[hi], send_sem=send_b.at[step], recv_sem=recv_b.at[hi],
            device_id={"gy": seat // 8, "gz_1": seat % 8}, device_id_type=MESH,
        )

    @pl.when(jnp.logical_not(is_root))
    def _():
        to_root(r).start()

    @pl.when(is_root)
    def _():
        acc = None
        slot_a[r] = partial
        for q in range(8):
            @pl.when(q != r)
            def _():
                to_root(q).wait_recv()
        for q in range(8):
            acc = slot_a[q] if q == 0 else acc + slot_a[q]
        sum_a[...] = acc
        slot_b[hi] = acc
        pl.semaphore_wait(ready, 2)

        @pl.loop(1, 32)
        def _(step):
            to_column(step).start()

    for q in range(4):
        @pl.when(jnp.logical_not(is_root & (hi == q)))
        def _():
            pltpu.make_async_remote_copy(
                src_ref=sum_a, dst_ref=slot_b.at[q], send_sem=send_b.at[0], recv_sem=recv_b.at[q],
                device_id={"gy": (hi + 1) % 4}, device_id_type=MESH,
            ).wait_recv()
    acc = slot_b[0]
    for q in range(1, 4):
        acc = acc + slot_b[q]
    sum_b[...] = acc

    def to_plane(n):
        return pltpu.make_async_remote_copy(
            src_ref=sum_b, dst_ref=slot_c.at[x * 8 + r], send_sem=send_c.at[n], recv_sem=recv_c.at[x * 8 + r],
            device_id=replica(n // 8, n % 8), device_id_type=MESH,
        )

    @pl.loop(1, 32)
    def _(n):
        to_plane(n).start()

    slot_c[x * 8 + r] = acc

    @pl.loop(1, 32)
    def _(n):
        other = ((x + n // 8) % 4) * 8 + (r + n % 8) % 8
        pltpu.make_async_remote_copy(
            src_ref=sum_b, dst_ref=slot_c.at[other], send_sem=send_c.at[n], recv_sem=recv_c.at[other],
            device_id=replica(n // 8, n % 8), device_id_type=MESH,
        ).wait_recv()

    slices = []
    for t in range(4):
        acc = slot_c[8 * t]
        for q in range(1, 8):
            acc = acc + slot_c[8 * t + q]
        slices.append(acc)
    quarter = lax.broadcasted_iota(I32, (4, 128), 1) // 32
    for q in range(4):
        rows = slices[0] if q == 0 else pltpu.roll(slices[0], (128 - 32 * q) % 128, 1)
        for t in range(1, 4):
            turned = slices[t] if t == q else pltpu.roll(slices[t], (128 + 32 * (t - q)) % 128, 1)
            rows = jnp.where(quarter == t, turned, rows)
        for m in range(3):
            if m * 4 + q < 9:
                out[m * 4 + q : m * 4 + q + 1, :] = rows[m : m + 1, :]

    @pl.when(jnp.logical_not(is_root))
    def _():
        to_root(r).wait_send()

    @pl.when(is_root)
    def _():
        @pl.loop(1, 32)
        def _(step):
            to_column(step).wait_send()

    @pl.loop(1, 32)
    def _(n):
        to_plane(n).wait_send()


def body(propagator, links, source_z, displacements, momenta, gamma_perm, gamma_phase):
    nz = lax.axis_size(GZ)
    sites_total = propagator.shape[6] * lax.axis_size("gy") * nz
    scaling = 1.0 / (24.0 * math.sqrt(sites_total))
    prop = jnp.transpose(propagator, (0, 2, 3, 1, 4, 5, 6)).reshape(288, 128)
    link = jnp.transpose(links, (1, 2, 0, 3, 4, 5)).reshape(9, 2, 128)
    smem = pl.BlockSpec(memory_space=pltpu.SMEM)
    hbm = pl.BlockSpec(memory_space=pl.ANY)
    dma = pltpu.SemaphoreType.DMA
    out = pl.pallas_call(
        functools.partial(kernel, nz, scaling),
        out_shape=jax.ShapeDtypeStruct((9, 128), F32),
        in_specs=[hbm, hbm, smem, smem, smem, smem, smem],
        out_specs=pl.BlockSpec(memory_space=pltpu.VMEM),
        scratch_shapes=[
            pltpu.VMEM((4, 288, 128), jnp.bfloat16),
            pltpu.VMEM((4, 9, 2, 128), jnp.bfloat16),
            pltpu.VMEM((4, 36, 8, 128), F32),
            pltpu.VMEM((3, 36, 8, 128), F32),
            pltpu.VMEM((3, 18, 8, 128), F32),
            pltpu.VMEM((3, 8, 8, 128), F32),
            pltpu.VMEM((3, 8, 128), I32),
            pltpu.VMEM((4, 128), F32),
            pltpu.VMEM((8, 4, 128), F32),
            pltpu.VMEM((4, 128), F32),
            pltpu.VMEM((4, 4, 128), F32),
            pltpu.VMEM((4, 128), F32),
            pltpu.VMEM((32, 4, 128), F32),
            dma((2,)),
            dma((6,)),
            dma((6,)),
            pltpu.SemaphoreType.REGULAR,
            dma,
            dma((8,)),
            dma((32,)),
            dma((4,)),
            dma((32,)),
            dma((32,)),
        ],
        compiler_params=pltpu.CompilerParams(collective_id=0, has_side_effects=True),
    )(prop, link, source_z, displacements, momenta, gamma_perm, gamma_phase)
    return jnp.transpose(out.reshape(9, 4, 4, 4, 2), (1, 0, 2, 3, 4))


def solution(mesh):
    torus = Mesh(
        mesh.devices.reshape(mesh.shape["ta"], 4, 8, 2, mesh.shape["gy"]),
        ("ta", "gz_0", "gz_1", "gz_2", "gy"),
    )
    in_specs = (
        P(None, None, None, None, "ta", GZ, "gy"),
        P(None, None, None, "ta", GZ, "gy"),
        P(),
        P(),
        P(),
        P(),
        P(),
    )
    return jax.shard_map(body, mesh=torus, in_specs=in_specs, out_specs=P(), check_vma=False)
```

time: 209 us -> 60.4 us (0.29)
  blocking collectives: 129 us -> 0 us
  Pallas kernels: 0 us -> 58.8 us
  starting transfers between devices: 25.1 us -> 0 us
  local copies, waits for them, and re-layouts: 19.8 us -> 1.43 us
  waiting for transfers between devices: 17.6 us -> 0 us
  other arithmetic: 9.52 us -> 0 us
  matrix products: 6.11 us -> 0 us
    psum x5 -> x0, blocking collectives: 129 us -> none  [over_axes(): array = lax.psum(array, axis)]
    pallas_call x0 -> x1, Pallas kernels: none -> 58.8 us  [body(): pl.pallas_call(functools.partial(kernel, nz, scaling), out_shape=jax.Shap...]
    all_to_all x2 -> x0, starting transfers between devices: 25.1 us -> none  [the longest x1 18.2 us: body(): lax.all_to_all(links[:, :, :, None], GZ, split_axis=6, concat_axis=5, til...]
    all_to_all x2 -> x0, waiting for transfers between devices: 17.6 us -> none  [the longest x1 11.4 us: body(): lax.all_to_all(propagator, GZ, split_axis=6, concat_axis=5, tiled=True)]
    dot_general x37 -> x0, matrix products: 6.11 us -> none  [the longest x36 5.87 us: contract(): jnp.einsum('tl,gl,pl->tgp', slice_weight, trace, table, precision=highest)]
    unnamed x59 -> x0, local copies, waits for them, and re-layouts: 5.54 us -> none
    another operation x19 -> x0, local copies, waits for them, and re-layouts: 4.12 us -> none  [the longest x10 2.05 us: project(): return jnp.stack([real_part, imag_part], axis=-1) * scaling]
    slice x14 -> x0, local copies, waits for them, and re-layouts: 4.08 us -> none  [the longest x2 2.13 us: spin_pairs(): source_real = source[0][:, None]]
  transfers between devices with their start and end apart: 2 -> 0, of which waited for: 2 -> 0; matrix products, arithmetic and copies ran while one was open for 6% -> 0% of each run, Pallas kernels for 0% -> 0%
where the time goes in v1:
time: 60.4 us; the launch traced here: 60.2 us
  Pallas kernels  58.8 us (97%)
  local copies, waits for them, and re-layouts  1.43 us (2%)
    pallas_call x1, Pallas kernels, body(): pl.pallas_call(functools.partial(kernel, nz, scaling), out_shape=jax.Shap...  58.8 us
    pallas_call x1, local copies, waits for them, and re-layouts, body(): pl.pallas_call(functools.partial(kernel, nz, scaling), out_shape=jax.Shap...  1.43 us

profile of v1, /device:TPU:1, one launch (start us, length us, event | category | flops | bytes accessed | tf_op | source)
XLA Modules:
  0.0 60.2 jit_solution(8980925486580582463)
XLA Ops:
  0.0 58.8 %shard_map.73 = f32[9,128]{1,0:T(8,128)} custom-call(bf16[288,128]{1,0:T(8,128)(2,1)} %bitcast.9, bf16[9,2,128]{2,1,0:T(2,128)(2,1)} %bitcast.10, s32[4,4]{1,0:T(4,128)} %source_z.1, s32[9]{0:T(128)} %displacements.1, s32[4]{0:T(128)} %momenta.1, s32[4,4]{1,0:T(4,128)} %perm.1, s32[4,4]{1,0:T(4,128)} %phase.1), custom_call_target="tpu_custom_call" | custom-call | tf_op jit(solution)/shard_map/pallas_call | solution.py:340
  58.8 1.4 %copy.9 = f32[9,128]{0,1:T(8,128)} copy(f32[9,128]{1,0:T(8,128)} %shard_map.73) | data formatting | bytes 9216 | tf_op jit(solution)/shard_map/pallas_call | solution.py:340

commit v2 on v1

--- a/solution.py
+++ b/solution.py
@@ -22,11 +22,16 @@
     return jnp.where(spin < 4 - r, pltpu.roll(x, 8 - r, 0), pltpu.roll(x, 4 - r, 0))
 
 
+ORDER = (1, 2, 3, 4, 5, 6, 7, 8, 31, 30, 29, 28, 27, 26, 25, 24, 9, 10, 11, 12, 13, 14, 15, 23, 22, 21, 20, 19, 18, 17, 16)
+
+
 def kernel(
-    nz, scaling, s_hbm, u_hbm, source_z, displacements, momenta, perm, phase, out,
-    sbuf, ubuf, left, fields, wil, table, kind, mine, slot_a, sum_a, slot_b, sum_b, slot_c,
-    load_sem, send_sem, recv_sem, ready, send_a, recv_a, send_b, recv_b, send_c, recv_c,
+    nz, scaling, s_hbm, u_hbm, *refs,
 ):
+    ints_hbm, out, ints = refs[:5], refs[5], refs[6:11]
+    sbuf, ubuf, left, fields, wil, table, kind, mine, slot_b, sum_b, slot_c, final = refs[11:23]
+    load_sem, send_sem, recv_sem, send_b, recv_b, send_c, recv_c, send_d, recv_d = refs[23:]
+    source_z, displacements, momenta, perm, phase = ints
     x = lax.axis_index("ta")
     gy0 = lax.axis_index("gz_0")
     lo = lax.axis_index("gz_1")
@@ -34,7 +39,8 @@
     hi = lax.axis_index("gy")
     z = gy0 * 16 + lo * 2 + core
     r = gy0 * 2 + core
-    is_root = r == lo
+    chip = hi * 8 + lo
+    is_centre = chip == 0
 
     def along(offset):
         w = (z + (offset + nz)) % nz
@@ -44,23 +50,44 @@
         q = (r + dr) % 8
         return {"ta": (x + dx) % 4, "gz_0": q // 2, "gz_2": q % 2}
 
-    load_s = pltpu.make_async_copy(s_hbm, sbuf.at[0], load_sem.at[0])
-    load_u = pltpu.make_async_copy(u_hbm, ubuf.at[0], load_sem.at[1])
-    load_s.start()
-    load_u.start()
+    loads = [pltpu.make_async_copy(s_hbm, sbuf.at[0], load_sem.at[0]), pltpu.make_async_copy(u_hbm, ubuf.at[0], load_sem.at[1])]
+    loads += [pltpu.make_async_copy(ints_hbm[n], ints[n], load_sem.at[2 + n]) for n in range(5)]
+    for load in loads:
+        load.start()
 
     barrier = pltpu.get_barrier_semaphore()
     for offset in (-2, -1, 1, 2):
         pl.semaphore_signal(barrier, inc=1, device_id=along(offset), device_id_type=MESH)
 
-    @pl.loop(1, 32)
-    def _(n):
-        pl.semaphore_signal(barrier, inc=1, device_id=replica(n // 8, n % 8), device_id_type=MESH)
-
-    lower = (hi + jnp.where(lo >= r, 0, 3)) % 4
-    for step in (0, 1):
-        seat = jnp.where(is_root, (hi + 3 + 2 * step) % 4, (lower + step) % 4)
-        pl.semaphore_signal(barrier, inc=1, device_id={"gy": seat, "gz_1": r}, device_id_type=MESH)
+    @pl.when(is_centre)
+    def _():
+        @pl.loop(1, 32)
+        def _(n):
+            pl.semaphore_signal(barrier, inc=1, device_id={"gy": n // 8, "gz_1": n % 8}, device_id_type=MESH)
+
+        @pl.loop(1, 32)
+        def _(n):
+            pl.semaphore_signal(barrier, inc=1, device_id=replica(n // 8, n % 8), device_id_type=MESH)
+
+    loads[0].wait()
+    loads[1].wait()
+    pl.semaphore_wait(barrier, jnp.where(is_centre, 35, 5))
+
+    def to(buf, n, dst, offset):
+        return pltpu.make_async_remote_copy(
+            src_ref=buf.at[0], dst_ref=buf.at[dst], send_sem=send_sem.at[n], recv_sem=recv_sem.at[n],
+            device_id=along(offset), device_id_type=MESH,
+        )
+
+    halo = [
+        to(sbuf, 0, 2, -2), to(sbuf, 1, 1, -1), to(sbuf, 2, 3, 2),
+        to(ubuf, 3, 1, -1), to(ubuf, 4, 2, 1), to(ubuf, 5, 3, 2),
+    ]
+    for n in (3, 4, 5, 0, 1, 2):
+        halo[n].start()
+
+    for load in loads[2:]:
+        load.wait()
 
     sub = lax.broadcasted_iota(I32, (8, 128), 0)
     lane = lax.broadcasted_iota(I32, (8, 128), 1)
@@ -109,35 +136,12 @@
                 value = jnp.where(h >= 2, -value, value)
                 table[m, rr * 2 + ri] = jnp.where(match & (j_id < 9), value, 0.0)
 
-    load_s.wait()
-    load_u.wait()
-
     @pl.loop(0, 18)
     def _(n):
         rows = sbuf[0, pl.ds(pl.multiple_of(n * 16, 16), 16), :].astype(F32)
         for half in range(2):
             for rr in range(4):
                 left[rr, 2 * n + half] = roll4(rows[half * 8 : half * 8 + 8], rr)
-
-    pl.semaphore_wait(barrier, 35 + jnp.where(is_root, 16, 0))
-
-    def to(buf, n, dst, offset):
-        return pltpu.make_async_remote_copy(
-            src_ref=buf.at[0], dst_ref=buf.at[dst], send_sem=send_sem.at[n], recv_sem=recv_sem.at[n],
-            device_id=along(offset), device_id_type=MESH,
-        )
-
-    halo = [
-        to(sbuf, 0, 2, -2), to(sbuf, 1, 1, -1), to(sbuf, 2, 3, 2),
-        to(ubuf, 3, 1, -1), to(ubuf, 4, 2, 1), to(ubuf, 5, 3, 2),
-    ]
-    for n in (3, 4, 5, 0, 1, 2):
-        halo[n].start()
-
-    @pl.when(is_root)
-    def _():
-        for step in (1, 3):
-            pl.semaphore_signal(ready, inc=1, device_id={"gy": (hi + step) % 4}, device_id_type=MESH)
 
     def link(slot):
         block = ubuf[slot].astype(F32)
@@ -230,52 +234,11 @@
 
     mine[...] = partial
 
-    def to_root(slot):
+    def to_centre():
         return pltpu.make_async_remote_copy(
-            src_ref=mine, dst_ref=slot_a.at[slot], send_sem=send_a, recv_sem=recv_a.at[slot],
-            device_id={"gz_0": lo // 2, "gz_2": lo % 2}, device_id_type=MESH,
+            src_ref=mine, dst_ref=slot_b.at[chip], send_sem=send_b, recv_sem=recv_b.at[chip],
+            device_id={"gy": 0, "gz_1": 0}, device_id_type=MESH,
         )
-
-    def to_column(step):
-        seat = (hi * 8 + lo + step) % 32
-        return pltpu.make_async_remote_copy(
-            src_ref=sum_a, dst_ref=slot_b.at[hi], send_sem=send_b.at[step], recv_sem=recv_b.at[hi],
-            device_id={"gy": seat // 8, "gz_1": seat % 8}, device_id_type=MESH,
-        )
-
-    @pl.when(jnp.logical_not(is_root))
-    def _():
-        to_root(r).start()
-
-    @pl.when(is_root)
-    def _():
-        acc = None
-        slot_a[r] = partial
-        for q in range(8):
-            @pl.when(q != r)
-            def _():
-                to_root(q).wait_recv()
-        for q in range(8):
-            acc = slot_a[q] if q == 0 else acc + slot_a[q]
-        sum_a[...] = acc
-        slot_b[hi] = acc
-        pl.semaphore_wait(ready, 2)
-
-        @pl.loop(1, 32)
-        def _(step):
-            to_column(step).start()
-
-    for q in range(4):
-        @pl.when(jnp.logical_not(is_root & (hi == q)))
-        def _():
-            pltpu.make_async_remote_copy(
-                src_ref=sum_a, dst_ref=slot_b.at[q], send_sem=send_b.at[0], recv_sem=recv_b.at[q],
-                device_id={"gy": (hi + 1) % 4}, device_id_type=MESH,
-            ).wait_recv()
-    acc = slot_b[0]
-    for q in range(1, 4):
-        acc = acc + slot_b[q]
-    sum_b[...] = acc
 
     def to_plane(n):
         return pltpu.make_async_remote_copy(
@@ -283,49 +246,87 @@
             device_id=replica(n // 8, n % 8), device_id_type=MESH,
         )
 
-    @pl.loop(1, 32)
-    def _(n):
-        to_plane(n).start()
-
-    slot_c[x * 8 + r] = acc
-
-    @pl.loop(1, 32)
-    def _(n):
-        other = ((x + n // 8) % 4) * 8 + (r + n % 8) % 8
-        pltpu.make_async_remote_copy(
-            src_ref=sum_b, dst_ref=slot_c.at[other], send_sem=send_c.at[n], recv_sem=recv_c.at[other],
-            device_id=replica(n // 8, n % 8), device_id_type=MESH,
-        ).wait_recv()
-
-    slices = []
-    for t in range(4):
-        acc = slot_c[8 * t]
-        for q in range(1, 8):
-            acc = acc + slot_c[8 * t + q]
-        slices.append(acc)
-    quarter = lax.broadcasted_iota(I32, (4, 128), 1) // 32
-    for q in range(4):
-        rows = slices[0] if q == 0 else pltpu.roll(slices[0], (128 - 32 * q) % 128, 1)
-        for t in range(1, 4):
-            turned = slices[t] if t == q else pltpu.roll(slices[t], (128 + 32 * (t - q)) % 128, 1)
-            rows = jnp.where(quarter == t, turned, rows)
-        for m in range(3):
-            if m * 4 + q < 9:
-                out[m * 4 + q : m * 4 + q + 1, :] = rows[m : m + 1, :]
-
-    @pl.when(jnp.logical_not(is_root))
-    def _():
-        to_root(r).wait_send()
-
-    @pl.when(is_root)
-    def _():
-        @pl.loop(1, 32)
-        def _(step):
-            to_column(step).wait_send()
-
-    @pl.loop(1, 32)
-    def _(n):
-        to_plane(n).wait_send()
+    def to_chip(n, dst):
+        return pltpu.make_async_remote_copy(
+            src_ref=final, dst_ref=final, send_sem=send_d.at[n], recv_sem=recv_d,
+            device_id={"gy": dst // 8, "gz_1": dst % 8}, device_id_type=MESH,
+        )
+
+    outward = (1, 2, 3, 4, 28, 8, 24, 12, 20, 16)
+
+    @pl.when(jnp.logical_not(is_centre))
+    def _():
+        to_centre().start()
+        to_chip(0, 0).wait_recv()
+
+        @pl.when(chip % 4 == 0)
+        def _():
+            for n in range(1, 4):
+                to_chip(n, chip + n).start()
+
+    @pl.when(is_centre)
+    def _():
+        acc = partial
+        for n in ORDER:
+            pltpu.make_async_remote_copy(
+                src_ref=mine, dst_ref=slot_b.at[n], send_sem=send_b, recv_sem=recv_b.at[n],
+                device_id={"gy": 1}, device_id_type=MESH,
+            ).wait_recv()
+            acc = acc + slot_b[n]
+        sum_b[...] = acc
+
+        @pl.loop(1, 32)
+        def _(n):
+            to_plane(n).start()
+
+        slot_c[x * 8 + r] = acc
+
+        @pl.loop(1, 32)
+        def _(n):
+            other = ((x + n // 8) % 4) * 8 + (r + n % 8) % 8
+            pltpu.make_async_remote_copy(
+                src_ref=sum_b, dst_ref=slot_c.at[other], send_sem=send_c.at[n], recv_sem=recv_c.at[other],
+                device_id=replica(n // 8, n % 8), device_id_type=MESH,
+            ).wait_recv()
+
+        slices = []
+        for t in range(4):
+            acc = slot_c[8 * t]
+            for q in range(1, 8):
+                acc = acc + slot_c[8 * t + q]
+            slices.append(acc)
+        quarter = lax.broadcasted_iota(I32, (4, 128), 1) // 32
+        for q in range(4):
+            rows = slices[0] if q == 0 else pltpu.roll(slices[0], (128 - 32 * q) % 128, 1)
+            for t in range(1, 4):
+                turned = slices[t] if t == q else pltpu.roll(slices[t], (128 + 32 * (t - q)) % 128, 1)
+                rows = jnp.where(quarter == t, turned, rows)
+            for m in range(3):
+                if m * 4 + q < 9:
+                    final[m * 4 + q] = rows[m : m + 1, :]
+        for n, dst in enumerate(outward):
+            to_chip(n, dst).start()
+
+    for j in range(9):
+        out[j : j + 1, :] = final[j]
+
+    @pl.when(jnp.logical_not(is_centre))
+    def _():
+        to_centre().wait_send()
+
+        @pl.when(chip % 4 == 0)
+        def _():
+            for n in range(1, 4):
+                to_chip(n, chip + n).wait_send()
+
+    @pl.when(is_centre)
+    def _():
+        @pl.loop(1, 32)
+        def _(n):
+            to_plane(n).wait_send()
+
+        for n, dst in enumerate(outward):
+            to_chip(n, dst).wait_send()
 
 
 def body(propagator, links, source_z, displacements, momenta, gamma_perm, gamma_phase):
@@ -334,15 +335,19 @@
     scaling = 1.0 / (24.0 * math.sqrt(sites_total))
     prop = jnp.transpose(propagator, (0, 2, 3, 1, 4, 5, 6)).reshape(288, 128)
     link = jnp.transpose(links, (1, 2, 0, 3, 4, 5)).reshape(9, 2, 128)
-    smem = pl.BlockSpec(memory_space=pltpu.SMEM)
     hbm = pl.BlockSpec(memory_space=pl.ANY)
     dma = pltpu.SemaphoreType.DMA
     out = pl.pallas_call(
         functools.partial(kernel, nz, scaling),
         out_shape=jax.ShapeDtypeStruct((9, 128), F32),
-        in_specs=[hbm, hbm, smem, smem, smem, smem, smem],
+        in_specs=[hbm] * 7,
         out_specs=pl.BlockSpec(memory_space=pltpu.VMEM),
         scratch_shapes=[
+            pltpu.SMEM((4, 4), I32),
+            pltpu.SMEM((9,), I32),
+            pltpu.SMEM((4,), I32),
+            pltpu.SMEM((4, 4), I32),
+            pltpu.SMEM((4, 4), I32),
             pltpu.VMEM((4, 288, 128), jnp.bfloat16),
             pltpu.VMEM((4, 9, 2, 128), jnp.bfloat16),
             pltpu.VMEM((4, 36, 8, 128), F32),
@@ -351,21 +356,19 @@
             pltpu.VMEM((3, 8, 8, 128), F32),
             pltpu.VMEM((3, 8, 128), I32),
             pltpu.VMEM((4, 128), F32),
-            pltpu.VMEM((8, 4, 128), F32),
-            pltpu.VMEM((4, 128), F32),
-            pltpu.VMEM((4, 4, 128), F32),
+            pltpu.VMEM((32, 4, 128), F32),
             pltpu.VMEM((4, 128), F32),
             pltpu.VMEM((32, 4, 128), F32),
-            dma((2,)),
+            pltpu.VMEM((9, 1, 128), F32),
+            dma((7,)),
             dma((6,)),
             dma((6,)),
-            pltpu.SemaphoreType.REGULAR,
             dma,
-            dma((8,)),
-            dma((32,)),
-            dma((4,)),
             dma((32,)),
             dma((32,)),
+            dma((32,)),
+            dma((10,)),
+            dma,
         ],
         compiler_params=pltpu.CompilerParams(collective_id=0, has_side_effects=True),
     )(prop, link, source_z, displacements, momenta, gamma_perm, gamma_phase)

time: 60.4 us -> 58.1 us (0.962)
  Pallas kernels: 58.8 us -> 56.5 us
    pallas_call x1, Pallas kernels: 58.8 us -> 56.5 us  [body(): pl.pallas_call(functools.partial(kernel, nz, scaling), out_shape=jax.Shap...]
where the time goes in v2:
time: 58.1 us; the launch traced here: 57.9 us
  Pallas kernels  56.5 us (97%)
  local copies, waits for them, and re-layouts  1.43 us (2%)
    pallas_call x1, Pallas kernels, body(): pl.pallas_call(functools.partial(kernel, nz, scaling), out_shape=jax.Shap...  56.5 us
    pallas_call x1, local copies, waits for them, and re-layouts, body(): pl.pallas_call(functools.partial(kernel, nz, scaling), out_shape=jax.Shap...  1.43 us

profile of v2, /device:TPU:1, one launch (start us, length us, event | category | flops | bytes accessed | tf_op | source)
XLA Modules:
  0.0 57.9 jit_solution(13093920807183637289)
XLA Ops:
  0.0 56.5 %shard_map.73 = f32[9,128]{1,0:T(8,128)} custom-call(bf16[288,128]{1,0:T(8,128)(2,1)} %bitcast.9, bf16[9,2,128]{2,1,0:T(2,128)(2,1)} %bitcast.10, s32[4,4]{1,0:T(4,128)} %refs_0_.1, s32[9]{0:T(128)} %refs_1_.1, s32[4]{0:T(128)} %refs_2_.1, s32[4,4]{1,0:T(4,128)} %refs_3_.1, s32[4,4]{1,0:T(4,128)} %refs_4_.1), custom_call_target="tpu_custom_call" | custom-call | tf_op jit(solution)/shard_map/pallas_call | solution.py:340
  56.5 1.4 %copy.9 = f32[9,128]{0,1:T(8,128)} copy(f32[9,128]{1,0:T(8,128)} %shard_map.73) | data formatting | bytes 9216 | tf_op jit(solution)/shard_map/pallas_call | solution.py:340

commit v3 on v2

--- a/solution.py
+++ b/solution.py
@@ -29,8 +29,8 @@
     nz, scaling, s_hbm, u_hbm, *refs,
 ):
     ints_hbm, out, ints = refs[:5], refs[5], refs[6:11]
-    sbuf, ubuf, left, fields, wil, table, kind, mine, slot_b, sum_b, slot_c, final = refs[11:23]
-    load_sem, send_sem, recv_sem, send_b, recv_b, send_c, recv_c, send_d, recv_d = refs[23:]
+    sbuf, ubuf, left, fields, wil, table, kind, mine, slot_b, sum_b, slot_c, final, xbuf, xlink, xfields, xwil, rot = refs[11:28]
+    load_sem, send_sem, recv_sem, send_b, recv_b, send_c, recv_c, send_d, recv_d, send_x, recv_x, recv_l = refs[28:]
     source_z, displacements, momenta, perm, phase = ints
     x = lax.axis_index("ta")
     gy0 = lax.axis_index("gz_0")
@@ -41,6 +41,16 @@
     r = gy0 * 2 + core
     chip = hi * 8 + lo
     is_centre = chip == 0
+    place = lo * 2 + core
+    at_end = hi >= 2
+    is_member = (place >= 12) | (place < 4)
+    member = jnp.where(place >= 12, place - 12, place + 4)
+    row_a = jnp.where(place >= 12, gy0, (gy0 + 3) % 4)
+    is_worker = jnp.where(at_end, place >= 13, place < 3)
+    first = jnp.where(at_end, 13, 0)
+
+    def seat(row, spot):
+        return {"gz_0": row % 4, "gz_1": spot // 2, "gz_2": spot % 2}
 
     def along(offset):
         w = (z + (offset + nz)) % nz
@@ -56,8 +66,20 @@
         load.start()
 
     barrier = pltpu.get_barrier_semaphore()
+    heard = jnp.where(is_centre, 31, 1) + jnp.where(is_member, 3, 0) - jnp.where(is_worker, 1, 0)
     for offset in (-2, -1, 1, 2):
-        pl.semaphore_signal(barrier, inc=1, device_id=along(offset), device_id_type=MESH)
+        inside = (place + offset >= 0) & (place + offset < 16)
+        heard = heard + jnp.where(inside, 1, 0)
+
+        @pl.when(inside)
+        def _():
+            pl.semaphore_signal(barrier, inc=1, device_id=along(offset), device_id_type=MESH)
+
+    for n in range(8):
+        @pl.when(is_worker & (n != member))
+        def _():
+            other = seat(row_a, 12 + n) if n < 4 else seat(row_a + 1, n - 4)
+            pl.semaphore_signal(barrier, inc=1, device_id=other, device_id_type=MESH)
 
     @pl.when(is_centre)
     def _():
@@ -71,7 +93,7 @@
 
     loads[0].wait()
     loads[1].wait()
-    pl.semaphore_wait(barrier, jnp.where(is_centre, 35, 5))
+    pl.semaphore_wait(barrier, heard)
 
     def to(buf, n, dst, offset):
         return pltpu.make_async_remote_copy(
@@ -83,8 +105,28 @@
         to(sbuf, 0, 2, -2), to(sbuf, 1, 1, -1), to(sbuf, 2, 3, 2),
         to(ubuf, 3, 1, -1), to(ubuf, 4, 2, 1), to(ubuf, 5, 3, 2),
     ]
+    offsets = (-2, -1, 2, -1, 1, 2)
+    goes = [(place + o >= 0) & (place + o < 16) for o in offsets]
+    comes = [(place - o >= 0) & (place - o < 16) for o in offsets]
+    for n in (3, 4, 5, 1, 0, 2):
+        pl.when(goes[n])(halo[n].start)
+
+    def to_worker(n):
+        third, spot = n % 3, first + n % 3
+        row = row_a + jnp.where(at_end, 0, 1)
+        src = sbuf.at[0, :, pl.ds(third * 16, 16), :] if n < 3 else ubuf.at[0]
+        dst, sem = (xbuf, recv_x) if n < 3 else (xlink, recv_l)
+        near = pltpu.make_async_copy(src, dst.at[member], sem.at[member])
+        far = pltpu.make_async_remote_copy(
+            src_ref=src, dst_ref=dst.at[member], send_sem=send_x.at[n], recv_sem=sem.at[member],
+            device_id=seat(row, spot), device_id_type=MESH,
+        )
+        return near, far, is_member & (place == spot), is_member & (place != spot)
+
     for n in (3, 4, 5, 0, 1, 2):
-        halo[n].start()
+        near, far, here, there = to_worker(n)
+        pl.when(here)(near.start)
+        pl.when(there)(far.start)
 
     for load in loads[2:]:
         load.wait()
@@ -107,6 +149,13 @@
     for p in range(4):
         mom = jnp.where(p_id == p, momenta[p], mom)
         src = jnp.where(p_id == p, source_z[x, p], src)
+    corner = jnp.where(at_end, 12 - place, -4 - place)
+    for n in range(5):
+        turns = (mom * (corner + n if n < 4 else -2)) & (nz - 1)
+        angle = turns.astype(F32) * (2.0 * math.pi / nz)
+        sine = jnp.sin(angle)
+        rot[n, 0] = jnp.cos(angle)
+        rot[n, 1] = jnp.where(c_id == 0, sine, -sine)
     for m in range(3):
         j_id = m * 4 + lane // 32
         shift = jnp.zeros((8, 128), I32)
@@ -114,7 +163,7 @@
             shift = jnp.where(j_id == j, displacements[j] - 4, shift)
         neg = shift < 0
         k_id = jnp.where(neg, -shift, shift)
-        at = z - jnp.where(k_id >= 3, 2, 0) + jnp.where(neg, k_id, 0)
+        at = z + jnp.where(neg, k_id, 0)
         turns = (mom * (at - src)) & (nz - 1)
         angle = turns.astype(F32) * (2.0 * math.pi / nz)
         cosine = jnp.cos(angle) * scaling
@@ -138,13 +187,13 @@
 
     @pl.loop(0, 18)
     def _(n):
-        rows = sbuf[0, pl.ds(pl.multiple_of(n * 16, 16), 16), :].astype(F32)
+        rows = sbuf[0, n // 3, pl.ds(pl.multiple_of(n % 3 * 16, 16), 16), :].astype(F32)
         for half in range(2):
             for rr in range(4):
                 left[rr, 2 * n + half] = roll4(rows[half * 8 : half * 8 + 8], rr)
 
-    def link(slot):
-        block = ubuf[slot].astype(F32)
+    def link(ref, slot):
+        block = ref[slot].astype(F32)
         return [
             [tuple(jnp.broadcast_to(block[3 * a + b, ri : ri + 1, :], (8, 128)) for ri in range(2)) for b in range(3)]
             for a in range(3)
@@ -161,78 +210,174 @@
 
         return [[entry(a, c) for c in range(3)] for a in range(3)]
 
-    for n in (3, 4, 5):
-        halo[n].wait()
-    base = link(0)
-    ahead = product(base, link(1))
-    back = product(link(3), link(2))
-    for a in range(3):
-        for b in range(3):
-            for ri in range(2):
-                wil[0, (a * 3 + b) * 2 + ri] = base[a][b][ri]
-                wil[1, (a * 3 + b) * 2 + ri] = ahead[a][b][ri]
-                wil[2, (a * 3 + b) * 2 + ri] = back[b][a][ri] if ri == 0 else -back[b][a][ri]
-
-    def transport(slot, line):
+    def keep(ref, line, matrix, dagger=False):
+        for a in range(3):
+            for b in range(3):
+                re, im = matrix[b][a] if dagger else matrix[a][b]
+                ref[line, (a * 3 + b) * 2] = re
+                ref[line, (a * 3 + b) * 2 + 1] = -im if dagger else im
+
+    def transport(load, lines, line, store):
+        got = [[load(ri * 3 + b) for ri in range(2)] for b in range(3)]
+        for half in range(2):
+            part = [[v[half * 8 : half * 8 + 8] for v in pair] for pair in got]
+            for a in range(3):
+                re = im = None
+                for b in range(3):
+                    if lines is None:
+                        re, im = part[a]
+                        break
+                    wr, wi = lines[line, (a * 3 + b) * 2], lines[line, (a * 3 + b) * 2 + 1]
+                    vr, vi = part[b]
+                    r2, i2 = wr * vr - wi * vi, wr * vi + wi * vr
+                    re, im = (r2, i2) if b == 0 else (re + r2, im + i2)
+                store(a, half, re, im)
+
+    def bring(slot, line):
         @pl.loop(0, 3)
         def _(q):
-            got = [
-                [sbuf[slot, pl.ds(pl.multiple_of((ri * 3 + b) * 48 + q * 16, 16), 16), :].astype(F32) for ri in range(2)]
-                for b in range(3)
-            ]
-            for half in range(2):
-                part = [[v[half * 8 : half * 8 + 8] for v in pair] for pair in got]
-                for a in range(3):
-                    re = im = None
-                    for b in range(3):
-                        wr, wi = wil[line, (a * 3 + b) * 2], wil[line, (a * 3 + b) * 2 + 1]
-                        vr, vi = part[b]
-                        r2, i2 = wr * vr - wi * vi, wr * vi + wi * vr
-                        re, im = (r2, i2) if b == 0 else (re + r2, im + i2)
-                    fields[line, a * 6 + q * 2 + half] = re
-                    fields[line, 18 + a * 6 + q * 2 + half] = im
-
-    halo[1].wait()
-    transport(1, 0)
-    halo[0].wait()
-    transport(2, 1)
-    halo[2].wait()
-    transport(3, 2)
+            def load(block):
+                return sbuf[slot, block, pl.ds(pl.multiple_of(q * 16, 16), 16), :].astype(F32)
+
+            def store(a, half, re, im):
+                fields[line, a * 6 + q * 2 + half] = re
+                fields[line, 18 + a * 6 + q * 2 + half] = im
+
+            transport(load, wil, line, store)
+
+    def clear(line):
+        @pl.loop(0, 36)
+        def _(n):
+            fields[line, n] = jnp.zeros((8, 128), F32)
+
+    keep(wil, 0, link(ubuf, 0))
+    for n in (3, 4, 5):
+        pl.when(comes[n])(halo[n].wait_recv)
+
+    @pl.when(comes[1])
+    def _():
+        halo[1].wait_recv()
+        bring(1, 0)
+
+    @pl.when(comes[0])
+    def _():
+        keep(wil, 1, product(link(ubuf, 0), link(ubuf, 1)))
+        halo[0].wait_recv()
+        bring(2, 1)
+
+    @pl.when(comes[2])
+    def _():
+        keep(wil, 2, product(link(ubuf, 3), link(ubuf, 2)), dagger=True)
+        halo[2].wait_recv()
+        bring(3, 2)
+
+    for line, n in ((0, 1), (1, 0), (2, 2)):
+        @pl.when(jnp.logical_not(comes[n]))
+        def _():
+            clear(line)
 
     kinds = [kind[m] for m in range(3)]
-    total = [jnp.zeros((8, 128), F32) for _ in range(3)]
+
+    def lane_sum(v):
+        return jnp.broadcast_to(jnp.sum(v, axis=1, keepdims=True), (8, 128))
+
+    def pick(lines, m):
+        value = jnp.zeros((8, 128), F32)
+        for k, line in lines.items():
+            value = jnp.where(kinds[m] == k, line, value)
+        return value
+
+    def turned(total, n):
+        rows = jnp.concatenate([jnp.sum(t, axis=0, keepdims=True) for t in total] + [jnp.zeros((1, 128), F32)], axis=0)
+        if n is None:
+            return rows
+        odd = lax.broadcasted_iota(I32, (4, 128), 1) % 2 == 1
+        swapped = jnp.where(odd, pltpu.roll(rows, 1, 1), pltpu.roll(rows, 127, 1))
+        return rows * rot[n, 0][0:4] + swapped * rot[n, 1][0:4]
+
+    def mac(acc, n, a_pair, b_pair):
+        (ar, ai), (br, bi) = a_pair, b_pair
+        acc[2 * n] = acc[2 * n] + (ar * br + ai * bi)
+        acc[2 * n + 1] = acc[2 * n + 1] + (ar * bi - ai * br)
+
+    total = [[jnp.zeros((8, 128), F32) for _ in range(3)] for _ in range(2)]
     for rr in range(4):
         def add(n, acc):
             acc = list(acc)
             for a in range(3):
                 re_at, im_at = n + 6 * a, 18 + n + 6 * a
-                sr, si = left[rr, re_at], left[rr, im_at]
-                lr, li = roll4(fields[2, re_at], rr), roll4(fields[2, im_at], rr)
-                right = [
-                    (left[0, re_at], left[0, im_at]),
-                    (fields[0, re_at], fields[0, im_at]),
-                    (fields[1, re_at], fields[1, im_at]),
-                ]
-                for k, ((ar, ai), (br, bi)) in enumerate(
-                    [((sr, si), right[0]), ((sr, si), right[1]), ((sr, si), right[2]), ((lr, li), right[1]), ((lr, li), right[2])]
-                ):
-                    acc[2 * k] = acc[2 * k] + (ar * br + ai * bi)
-                    acc[2 * k + 1] = acc[2 * k + 1] + (ar * bi - ai * br)
+                here = (left[rr, re_at], left[rr, im_at])
+                behind = (roll4(fields[2, re_at], rr), roll4(fields[2, im_at], rr))
+                one, two = (fields[0, re_at], fields[0, im_at]), (fields[1, re_at], fields[1, im_at])
+                mac(acc, 0, here, (left[0, re_at], left[0, im_at]))
+                mac(acc, 1, here, one)
+                mac(acc, 2, here, two)
+                mac(acc, 3, behind, one)
+                mac(acc, 4, behind, two)
             return tuple(acc)
 
         sums = lax.fori_loop(0, 6, add, tuple(jnp.zeros((8, 128), F32) for _ in range(10)))
         for ri in range(2):
-            lines = [jnp.broadcast_to(jnp.sum(sums[2 * k + ri], axis=1, keepdims=True), (8, 128)) for k in range(5)]
+            lines = {k: lane_sum(sums[2 * k + ri]) for k in range(5)}
             for m in range(3):
-                value = lines[0]
-                for k in range(1, 5):
-                    value = jnp.where(kinds[m] == k, lines[k], value)
-                total[m] = total[m] + table[m, rr * 2 + ri] * value
-    flat = [jnp.sum(t, axis=0, keepdims=True) for t in total]
-    flat.append(jnp.zeros((1, 128), F32))
-    partial = jnp.concatenate(flat, axis=0)
-
-    mine[...] = partial
+                entry = table[m, rr * 2 + ri]
+                total[0][m] = total[0][m] + entry * pick({k: lines[k] for k in (0, 1, 2)}, m)
+                total[1][m] = total[1][m] + entry * pick({k: lines[k] for k in (3, 4)}, m)
+    mine[...] = turned(total[0], None) + turned(total[1], 4)
+
+    @pl.when(is_worker)
+    def _():
+        def arrived(n, dst, sem):
+            return pltpu.make_async_remote_copy(
+                src_ref=dst.at[n], dst_ref=dst.at[n], send_sem=send_x.at[0], recv_sem=sem.at[n],
+                device_id=seat(gy0 + 1, place), device_id_type=MESH,
+            )
+
+        for n in range(8):
+            arrived(n, xlink, recv_l).wait_recv()
+        line = link(xlink, 3)
+        keep(xwil, 3, line, dagger=True)
+        for n in (2, 1, 0):
+            line = product(link(xlink, n), line)
+            keep(xwil, n, line, dagger=True)
+        line = link(xlink, 4)
+        keep(xwil, 4, line)
+        for n in (5, 6):
+            line = product(line, link(xlink, n))
+            keep(xwil, n, line)
+        for n in range(8):
+            arrived(n, xbuf, recv_x).wait_recv()
+
+            def load(block):
+                return xbuf[n, block].astype(F32)
+
+            def store(a, half, re, im):
+                xfields[n, a * 2 + half] = re
+                xfields[n, 6 + a * 2 + half] = im
+
+            transport(load, None if n == 4 else xwil, n if n < 4 else n - 1, store)
+
+        cross = [(i, j) for i in range(4) for j in range(i + 1)]
+        total = [[jnp.zeros((8, 128), F32) for _ in range(3)] for _ in range(4)]
+        for rr in range(4):
+            def add(n, acc):
+                acc = list(acc)
+                ahead = [(xfields[4 + j, n], xfields[4 + j, 6 + n]) for j in range(4)]
+                for i in range(4):
+                    behind = (roll4(xfields[i, n], rr), roll4(xfields[i, 6 + n], rr))
+                    for j in range(i + 1):
+                        mac(acc, cross.index((i, j)), behind, ahead[j])
+                return tuple(acc)
+
+            sums = lax.fori_loop(0, 6, add, tuple(jnp.zeros((8, 128), F32) for _ in range(20)))
+            for ri in range(2):
+                lines = [lane_sum(sums[2 * n + ri]) for n in range(10)]
+                for m in range(3):
+                    entry = table[m, rr * 2 + ri]
+                    for i in range(4):
+                        at_k = {4 - i + j: lines[cross.index((i, j))] for j in range(i + 1)}
+                        total[i][m] = total[i][m] + entry * pick(at_k, m)
+        mine[...] = mine[...] + ((turned(total[0], 0) + turned(total[1], 1)) + (turned(total[2], 2) + turned(total[3], 3)))
 
     def to_centre():
         return pltpu.make_async_remote_copy(
@@ -266,7 +411,7 @@
 
     @pl.when(is_centre)
     def _():
-        acc = partial
+        acc = mine[...]
         for n in ORDER:
             pltpu.make_async_remote_copy(
                 src_ref=mine, dst_ref=slot_b.at[n], send_sem=send_b, recv_sem=recv_b.at[n],
@@ -310,6 +455,12 @@
     for j in range(9):
         out[j : j + 1, :] = final[j]
 
+    for n in range(6):
+        pl.when(goes[n])(halo[n].wait_send)
+    for n in range(6):
+        _, far, _, there = to_worker(n)
+        pl.when(there)(far.wait_send)
+
     @pl.when(jnp.logical_not(is_centre))
     def _():
         to_centre().wait_send()
@@ -333,7 +484,7 @@
     nz = lax.axis_size(GZ)
     sites_total = propagator.shape[6] * lax.axis_size("gy") * nz
     scaling = 1.0 / (24.0 * math.sqrt(sites_total))
-    prop = jnp.transpose(propagator, (0, 2, 3, 1, 4, 5, 6)).reshape(288, 128)
+    prop = jnp.transpose(propagator, (0, 2, 3, 1, 4, 5, 6)).reshape(6, 48, 128)
     link = jnp.transpose(links, (1, 2, 0, 3, 4, 5)).reshape(9, 2, 128)
     hbm = pl.BlockSpec(memory_space=pl.ANY)
     dma = pltpu.SemaphoreType.DMA
@@ -348,7 +499,7 @@
             pltpu.SMEM((4,), I32),
             pltpu.SMEM((4, 4), I32),
             pltpu.SMEM((4, 4), I32),
-            pltpu.VMEM((4, 288, 128), jnp.bfloat16),
+            pltpu.VMEM((4, 6, 48, 128), jnp.bfloat16),
             pltpu.VMEM((4, 9, 2, 128), jnp.bfloat16),
             pltpu.VMEM((4, 36, 8, 128), F32),
             pltpu.VMEM((3, 36, 8, 128), F32),
@@ -360,6 +511,11 @@
             pltpu.VMEM((4, 128), F32),
             pltpu.VMEM((32, 4, 128), F32),
             pltpu.VMEM((9, 1, 128), F32),
+            pltpu.VMEM((8, 6, 16, 128), jnp.bfloat16),
+            pltpu.VMEM((8, 9, 2, 128), jnp.bfloat16),
+            pltpu.VMEM((8, 12, 8, 128), F32),
+            pltpu.VMEM((7, 18, 8, 128), F32),
+            pltpu.VMEM((5, 2, 8, 128), F32),
             dma((7,)),
             dma((6,)),
             dma((6,)),
@@ -369,6 +525,9 @@
             dma((32,)),
             dma((10,)),
             dma,
+            dma((6,)),
+            dma((8,)),
+            dma((8,)),
         ],
         compiler_params=pltpu.CompilerParams(collective_id=0, has_side_effects=True),
     )(prop, link, source_z, displacements, momenta, gamma_perm, gamma_phase)

time: 58.1 us -> 55.7 us (0.959)
  Pallas kernels: 56.5 us -> 54.1 us
    pallas_call x1, Pallas kernels: 56.5 us -> 54.1 us  [body(): pl.pallas_call(functools.partial(kernel, nz, scaling), out_shape=jax.Shap...]
where the time goes in v3:
time: 55.7 us; the launch traced here: 55.5 us
  Pallas kernels  54.1 us (97%)
  local copies, waits for them, and re-layouts  1.43 us (3%)
    pallas_call x1, Pallas kernels, body(): pl.pallas_call(functools.partial(kernel, nz, scaling), out_shape=jax.Shap...  54.1 us
    pallas_call x1, local copies, waits for them, and re-layouts, body(): pl.pallas_call(functools.partial(kernel, nz, scaling), out_shape=jax.Shap...  1.43 us

profile of v3, /device:TPU:1, one launch (start us, length us, event | category | flops | bytes accessed | tf_op | source)
XLA Modules:
  0.0 55.5 jit_solution(3260798052434106487)
XLA Ops:
  0.0 54.1 %shard_map.73 = f32[9,128]{1,0:T(8,128)} custom-call(bf16[6,48,128]{2,1,0:T(8,128)(2,1)} %bitcast.9, bf16[9,2,128]{2,1,0:T(2,128)(2,1)} %bitcast.10, s32[4,4]{1,0:T(4,128)} %refs_0_.1, s32[9]{0:T(128)} %refs_1_.1, s32[4]{0:T(128)} %refs_2_.1, s32[4,4]{1,0:T(4,128)} %refs_3_.1, s32[4,4]{1,0:T(4,128)} %refs_4_.1), custom_call_target="tpu_custom_call" | custom-call | tf_op jit(solution)/shard_map/pallas_call | solution.py:491
  54.1 1.4 %copy.9 = f32[9,128]{0,1:T(8,128)} copy(f32[9,128]{1,0:T(8,128)} %shard_map.73) | data formatting | bytes 9216 | tf_op jit(solution)/shard_map/pallas_call | solution.py:491

commit v4 on v3

--- a/solution.py
+++ b/solution.py
@@ -20,9 +20,6 @@
         return x
     spin = lax.broadcasted_iota(I32, (8, 128), 0) % 4
     return jnp.where(spin < 4 - r, pltpu.roll(x, 8 - r, 0), pltpu.roll(x, 4 - r, 0))
-
-
-ORDER = (1, 2, 3, 4, 5, 6, 7, 8, 31, 30, 29, 28, 27, 26, 25, 24, 9, 10, 11, 12, 13, 14, 15, 23, 22, 21, 20, 19, 18, 17, 16)
 
 
 def kernel(
@@ -111,14 +108,20 @@
     for n in (3, 4, 5, 1, 0, 2):
         pl.when(goes[n])(halo[n].start)
 
+    def bulk(ref, sem):
+        return pltpu.make_async_remote_copy(
+            src_ref=ref, dst_ref=ref, send_sem=sem, recv_sem=sem, device_id={"gy": (hi + 1) % 4}, device_id_type=MESH
+        )
+
     def to_worker(n):
         third, spot = n % 3, first + n % 3
         row = row_a + jnp.where(at_end, 0, 1)
         src = sbuf.at[0, :, pl.ds(third * 16, 16), :] if n < 3 else ubuf.at[0]
         dst, sem = (xbuf, recv_x) if n < 3 else (xlink, recv_l)
-        near = pltpu.make_async_copy(src, dst.at[member], sem.at[member])
+        side = jnp.where(place >= 12, 0, 1)
+        near = pltpu.make_async_copy(src, dst.at[member], sem.at[side])
         far = pltpu.make_async_remote_copy(
-            src_ref=src, dst_ref=dst.at[member], send_sem=send_x.at[n], recv_sem=sem.at[member],
+            src_ref=src, dst_ref=dst.at[member], send_sem=send_x.at[n // 3], recv_sem=sem.at[side],
             device_id=seat(row, spot), device_id_type=MESH,
         )
         return near, far, is_member & (place == spot), is_member & (place != spot)
@@ -192,6 +195,53 @@
             for rr in range(4):
                 left[rr, 2 * n + half] = roll4(rows[half * 8 : half * 8 + 8], rr)
 
+    kinds = [kind[m] for m in range(3)]
+
+    def lane_sum(v):
+        return jnp.broadcast_to(jnp.sum(v, axis=1, keepdims=True), (8, 128))
+
+    def pick(lines, m):
+        value = jnp.zeros((8, 128), F32)
+        for k, line in lines.items():
+            value = jnp.where(kinds[m] == k, line, value)
+        return value
+
+    def turned(total, n):
+        rows = jnp.concatenate([jnp.sum(t, axis=0, keepdims=True) for t in total] + [jnp.zeros((1, 128), F32)], axis=0)
+        if n is None:
+            return rows
+        odd = lax.broadcasted_iota(I32, (4, 128), 1) % 2 == 1
+        swapped = jnp.where(odd, pltpu.roll(rows, 1, 1), pltpu.roll(rows, 127, 1))
+        return rows * rot[n, 0][0:4] + swapped * rot[n, 1][0:4]
+
+    def mac(acc, n, a_pair, b_pair):
+        (ar, ai), (br, bi) = a_pair, b_pair
+        acc[2 * n] = acc[2 * n] + (ar * br + ai * bi)
+        acc[2 * n + 1] = acc[2 * n + 1] + (ar * bi - ai * br)
+
+    total = [[jnp.zeros((8, 128), F32) for _ in range(3)] for _ in range(2)]
+
+    def own_pairs(rr, n, acc):
+        acc = list(acc)
+        for a in range(3):
+            re_at, im_at = n + 6 * a, 18 + n + 6 * a
+            mac(acc, 0, (left[rr, re_at], left[rr, im_at]), (left[0, re_at], left[0, im_at]))
+        return tuple(acc)
+
+    def regular(kinds_at, add, groups, total):
+        for rr in range(4):
+            zero = tuple(jnp.zeros((8, 128), F32) for _ in range(2 * len(kinds_at)))
+            sums = lax.fori_loop(0, 6, functools.partial(add, rr), zero, unroll=True)
+            for ri in range(2):
+                lines = {k: lane_sum(sums[2 * n + ri]) for n, k in enumerate(kinds_at)}
+                for m in range(3):
+                    entry = table[m, rr * 2 + ri]
+                    for g, ks in enumerate(groups):
+                        if ks:
+                            total[g][m] = total[g][m] + entry * pick({k: lines[k] for k in ks}, m)
+
+    regular((0,), own_pairs, ((0,), ()), total)
+
     def link(ref, slot):
         block = ref[slot].astype(F32)
         return [
@@ -276,86 +326,52 @@
         def _():
             clear(line)
 
-    kinds = [kind[m] for m in range(3)]
-
-    def lane_sum(v):
-        return jnp.broadcast_to(jnp.sum(v, axis=1, keepdims=True), (8, 128))
-
-    def pick(lines, m):
-        value = jnp.zeros((8, 128), F32)
-        for k, line in lines.items():
-            value = jnp.where(kinds[m] == k, line, value)
-        return value
-
-    def turned(total, n):
-        rows = jnp.concatenate([jnp.sum(t, axis=0, keepdims=True) for t in total] + [jnp.zeros((1, 128), F32)], axis=0)
-        if n is None:
-            return rows
-        odd = lax.broadcasted_iota(I32, (4, 128), 1) % 2 == 1
-        swapped = jnp.where(odd, pltpu.roll(rows, 1, 1), pltpu.roll(rows, 127, 1))
-        return rows * rot[n, 0][0:4] + swapped * rot[n, 1][0:4]
-
-    def mac(acc, n, a_pair, b_pair):
-        (ar, ai), (br, bi) = a_pair, b_pair
-        acc[2 * n] = acc[2 * n] + (ar * br + ai * bi)
-        acc[2 * n + 1] = acc[2 * n + 1] + (ar * bi - ai * br)
-
-    total = [[jnp.zeros((8, 128), F32) for _ in range(3)] for _ in range(2)]
-    for rr in range(4):
-        def add(n, acc):
-            acc = list(acc)
-            for a in range(3):
-                re_at, im_at = n + 6 * a, 18 + n + 6 * a
-                here = (left[rr, re_at], left[rr, im_at])
-                behind = (roll4(fields[2, re_at], rr), roll4(fields[2, im_at], rr))
-                one, two = (fields[0, re_at], fields[0, im_at]), (fields[1, re_at], fields[1, im_at])
-                mac(acc, 0, here, (left[0, re_at], left[0, im_at]))
-                mac(acc, 1, here, one)
-                mac(acc, 2, here, two)
-                mac(acc, 3, behind, one)
-                mac(acc, 4, behind, two)
-            return tuple(acc)
-
-        sums = lax.fori_loop(0, 6, add, tuple(jnp.zeros((8, 128), F32) for _ in range(10)))
-        for ri in range(2):
-            lines = {k: lane_sum(sums[2 * k + ri]) for k in range(5)}
-            for m in range(3):
-                entry = table[m, rr * 2 + ri]
-                total[0][m] = total[0][m] + entry * pick({k: lines[k] for k in (0, 1, 2)}, m)
-                total[1][m] = total[1][m] + entry * pick({k: lines[k] for k in (3, 4)}, m)
+    def moved_pairs(rr, n, acc):
+        acc = list(acc)
+        for a in range(3):
+            re_at, im_at = n + 6 * a, 18 + n + 6 * a
+            here = (left[rr, re_at], left[rr, im_at])
+            behind = (roll4(fields[2, re_at], rr), roll4(fields[2, im_at], rr))
+            one, two = (fields[0, re_at], fields[0, im_at]), (fields[1, re_at], fields[1, im_at])
+            mac(acc, 0, here, one)
+            mac(acc, 1, here, two)
+            mac(acc, 2, behind, one)
+            mac(acc, 3, behind, two)
+        return tuple(acc)
+
+    regular((1, 2, 3, 4), moved_pairs, ((1, 2), (3, 4)), total)
     mine[...] = turned(total[0], None) + turned(total[1], 4)
 
     @pl.when(is_worker)
     def _():
-        def arrived(n, dst, sem):
-            return pltpu.make_async_remote_copy(
-                src_ref=dst.at[n], dst_ref=dst.at[n], send_sem=send_x.at[0], recv_sem=sem.at[n],
-                device_id=seat(gy0 + 1, place), device_id_type=MESH,
-            )
-
-        for n in range(8):
-            arrived(n, xlink, recv_l).wait_recv()
+        def bring_cross(n, line):
+            def load(block):
+                return xbuf[n, block].astype(F32)
+
+            def store(a, half, re, im):
+                xfields[n, a * 2 + half] = re
+                xfields[n, 6 + a * 2 + half] = im
+
+            transport(load, None if line is None else xwil, line, store)
+
+        bulk(xlink.at[pl.ds(0, 4)], recv_l.at[0]).wait_recv()
         line = link(xlink, 3)
         keep(xwil, 3, line, dagger=True)
         for n in (2, 1, 0):
             line = product(link(xlink, n), line)
             keep(xwil, n, line, dagger=True)
+        bulk(xbuf.at[pl.ds(0, 4)], recv_x.at[0]).wait_recv()
+        for n in range(4):
+            bring_cross(n, n)
+        bulk(xlink.at[pl.ds(4, 4)], recv_l.at[1]).wait_recv()
         line = link(xlink, 4)
         keep(xwil, 4, line)
         for n in (5, 6):
             line = product(line, link(xlink, n))
             keep(xwil, n, line)
-        for n in range(8):
-            arrived(n, xbuf, recv_x).wait_recv()
-
-            def load(block):
-                return xbuf[n, block].astype(F32)
-
-            def store(a, half, re, im):
-                xfields[n, a * 2 + half] = re
-                xfields[n, 6 + a * 2 + half] = im
-
-            transport(load, None if n == 4 else xwil, n if n < 4 else n - 1, store)
+        bulk(xbuf.at[pl.ds(4, 4)], recv_x.at[1]).wait_recv()
+        for n in range(4, 8):
+            bring_cross(n, None if n == 4 else n - 1)
 
         cross = [(i, j) for i in range(4) for j in range(i + 1)]
         total = [[jnp.zeros((8, 128), F32) for _ in range(3)] for _ in range(4)]
@@ -369,7 +385,7 @@
                         mac(acc, cross.index((i, j)), behind, ahead[j])
                 return tuple(acc)
 
-            sums = lax.fori_loop(0, 6, add, tuple(jnp.zeros((8, 128), F32) for _ in range(20)))
+            sums = lax.fori_loop(0, 6, add, tuple(jnp.zeros((8, 128), F32) for _ in range(20)), unroll=True)
             for ri in range(2):
                 lines = [lane_sum(sums[2 * n + ri]) for n in range(10)]
                 for m in range(3):
@@ -381,59 +397,47 @@
 
     def to_centre():
         return pltpu.make_async_remote_copy(
-            src_ref=mine, dst_ref=slot_b.at[chip], send_sem=send_b, recv_sem=recv_b.at[chip],
+            src_ref=mine, dst_ref=slot_b.at[chip], send_sem=send_b, recv_sem=recv_b,
             device_id={"gy": 0, "gz_1": 0}, device_id_type=MESH,
         )
 
     def to_plane(n):
         return pltpu.make_async_remote_copy(
-            src_ref=sum_b, dst_ref=slot_c.at[x * 8 + r], send_sem=send_c.at[n], recv_sem=recv_c.at[x * 8 + r],
-            device_id=replica(n // 8, n % 8), device_id_type=MESH,
+            src_ref=sum_b, dst_ref=slot_c.at[x * 8 + r], send_sem=send_c, recv_sem=recv_c,
+            device_id={"ta": n // 8, "gz_0": n % 8 // 2, "gz_2": n % 2}, device_id_type=MESH,
         )
 
-    def to_chip(n, dst):
+    def to_chip(dst):
         return pltpu.make_async_remote_copy(
-            src_ref=final, dst_ref=final, send_sem=send_d.at[n], recv_sem=recv_d,
+            src_ref=final.at[0], dst_ref=final.at[0], send_sem=send_d, recv_sem=recv_d,
             device_id={"gy": dst // 8, "gz_1": dst % 8}, device_id_type=MESH,
         )
 
-    outward = (1, 2, 3, 4, 28, 8, 24, 12, 20, 16)
+    outward = (1, 2, 3, 4, 5, 6, 7, 28, 8, 24, 12, 20, 16)
+    is_head = (chip % 4 == 0) & (chip >= 8)
 
     @pl.when(jnp.logical_not(is_centre))
     def _():
         to_centre().start()
-        to_chip(0, 0).wait_recv()
-
-        @pl.when(chip % 4 == 0)
+        to_chip(0).wait_recv()
+
+        @pl.when(is_head)
         def _():
             for n in range(1, 4):
-                to_chip(n, chip + n).start()
+                to_chip(chip + n).start()
 
     @pl.when(is_centre)
     def _():
         acc = mine[...]
-        for n in ORDER:
-            pltpu.make_async_remote_copy(
-                src_ref=mine, dst_ref=slot_b.at[n], send_sem=send_b, recv_sem=recv_b.at[n],
-                device_id={"gy": 1}, device_id_type=MESH,
-            ).wait_recv()
+        bulk(slot_b.at[pl.ds(1, 31)], recv_b).wait_recv()
+        for n in range(1, 32):
             acc = acc + slot_b[n]
         sum_b[...] = acc
 
-        @pl.loop(1, 32)
-        def _(n):
-            to_plane(n).start()
-
+        for n in range(32):
+            pl.when(x * 8 + r != n)(to_plane(n).start)
         slot_c[x * 8 + r] = acc
-
-        @pl.loop(1, 32)
-        def _(n):
-            other = ((x + n // 8) % 4) * 8 + (r + n % 8) % 8
-            pltpu.make_async_remote_copy(
-                src_ref=sum_b, dst_ref=slot_c.at[other], send_sem=send_c.at[n], recv_sem=recv_c.at[other],
-                device_id=replica(n // 8, n % 8), device_id_type=MESH,
-            ).wait_recv()
-
+        bulk(slot_c.at[pl.ds(0, 31)], recv_c).wait_recv()
         slices = []
         for t in range(4):
             acc = slot_c[8 * t]
@@ -448,36 +452,37 @@
                 rows = jnp.where(quarter == t, turned, rows)
             for m in range(3):
                 if m * 4 + q < 9:
-                    final[m * 4 + q] = rows[m : m + 1, :]
-        for n, dst in enumerate(outward):
-            to_chip(n, dst).start()
+                    final[0, m * 4 + q] = rows[m : m + 1, :]
+        for dst in outward:
+            to_chip(dst).start()
 
     for j in range(9):
-        out[j : j + 1, :] = final[j]
+        out[j : j + 1, :] = final[0, j]
 
     for n in range(6):
         pl.when(goes[n])(halo[n].wait_send)
-    for n in range(6):
-        _, far, _, there = to_worker(n)
-        pl.when(there)(far.wait_send)
+    @pl.when(is_member & is_worker)
+    def _():
+        bulk(sbuf.at[0, :, pl.ds(0, 32), :], send_x.at[0]).wait_send()
+        bulk(ubuf.at[pl.ds(0, 2)], send_x.at[1]).wait_send()
+
+    @pl.when(is_member & jnp.logical_not(is_worker))
+    def _():
+        bulk(sbuf.at[0], send_x.at[0]).wait_send()
+        bulk(ubuf.at[pl.ds(0, 3)], send_x.at[1]).wait_send()
 
     @pl.when(jnp.logical_not(is_centre))
     def _():
         to_centre().wait_send()
 
-        @pl.when(chip % 4 == 0)
+        @pl.when(is_head)
         def _():
-            for n in range(1, 4):
-                to_chip(n, chip + n).wait_send()
+            bulk(final.at[pl.ds(0, 3)], send_d).wait_send()
 
     @pl.when(is_centre)
     def _():
-        @pl.loop(1, 32)
-        def _(n):
-            to_plane(n).wait_send()
-
-        for n, dst in enumerate(outward):
-            to_chip(n, dst).wait_send()
+        bulk(slot_c.at[pl.ds(0, 31)], send_c).wait_send()
+        bulk(final, send_d).wait_send()
 
 
 def body(propagator, links, source_z, displacements, momenta, gamma_perm, gamma_phase):
@@ -510,7 +515,7 @@
             pltpu.VMEM((32, 4, 128), F32),
             pltpu.VMEM((4, 128), F32),
             pltpu.VMEM((32, 4, 128), F32),
-            pltpu.VMEM((9, 1, 128), F32),
+            pltpu.VMEM((13, 9, 1, 128), F32),
             pltpu.VMEM((8, 6, 16, 128), jnp.bfloat16),
             pltpu.VMEM((8, 9, 2, 128), jnp.bfloat16),
             pltpu.VMEM((8, 12, 8, 128), F32),
@@ -520,14 +525,14 @@
             dma((6,)),
             dma((6,)),
             dma,
-            dma((32,)),
-            dma((32,)),
-            dma((32,)),
-            dma((10,)),
             dma,
-            dma((6,)),
-            dma((8,)),
-            dma((8,)),
+            dma,
+            dma,
+            dma,
+            dma,
+            dma((2,)),
+            dma((2,)),
+            dma((2,)),
         ],
         compiler_params=pltpu.CompilerParams(collective_id=0, has_side_effects=True),
     )(prop, link, source_z, displacements, momenta, gamma_perm, gamma_phase)

time: 55.7 us -> 53.8 us (0.966)
  Pallas kernels: 54.1 us -> 52.2 us
    pallas_call x1, Pallas kernels: 54.1 us -> 52.2 us  [body(): pl.pallas_call(functools.partial(kernel, nz, scaling), out_shape=jax.Shap...]
where the time goes in v4:
time: 53.8 us; the launch traced here: 53.6 us
  Pallas kernels  52.2 us (97%)
  local copies, waits for them, and re-layouts  1.43 us (3%)
    pallas_call x1, Pallas kernels, body(): pl.pallas_call(functools.partial(kernel, nz, scaling), out_shape=jax.Shap...  52.2 us
    pallas_call x1, local copies, waits for them, and re-layouts, body(): pl.pallas_call(functools.partial(kernel, nz, scaling), out_shape=jax.Shap...  1.43 us

profile of v4, /device:TPU:1, one launch (start us, length us, event | category | flops | bytes accessed | tf_op | source)
XLA Modules:
  0.0 53.6 jit_solution(15758416041580636908)
XLA Ops:
  0.0 52.2 %shard_map.73 = f32[9,128]{1,0:T(8,128)} custom-call(bf16[6,48,128]{2,1,0:T(8,128)(2,1)} %bitcast.9, bf16[9,2,128]{2,1,0:T(2,128)(2,1)} %bitcast.10, s32[4,4]{1,0:T(4,128)} %refs_0_.1, s32[9]{0:T(128)} %refs_1_.1, s32[4]{0:T(128)} %refs_2_.1, s32[4,4]{1,0:T(4,128)} %refs_3_.1, s32[4,4]{1,0:T(4,128)} %refs_4_.1), custom_call_target="tpu_custom_call" | custom-call | tf_op jit(solution)/shard_map/pallas_call | solution.py:496
  52.2 1.4 %copy.9 = f32[9,128]{0,1:T(8,128)} copy(f32[9,128]{1,0:T(8,128)} %shard_map.73) | data formatting | bytes 9216 | tf_op jit(solution)/shard_map/pallas_call | solution.py:496

commit v5 on v4

--- a/solution.py
+++ b/solution.py
@@ -35,9 +35,9 @@
     core = lax.axis_index("gz_2")
     hi = lax.axis_index("gy")
     z = gy0 * 16 + lo * 2 + core
-    r = gy0 * 2 + core
     chip = hi * 8 + lo
-    is_centre = chip == 0
+    is_centre = (chip == 0) & (core == 1)
+    column = x * 4 + gy0
     place = lo * 2 + core
     at_end = hi >= 2
     is_member = (place >= 12) | (place < 4)
@@ -53,17 +53,13 @@
         w = (z + (offset + nz)) % nz
         return {"gz_0": w // 16, "gz_1": (w // 2) % 8, "gz_2": w % 2}
 
-    def replica(dx, dr):
-        q = (r + dr) % 8
-        return {"ta": (x + dx) % 4, "gz_0": q // 2, "gz_2": q % 2}
-
     loads = [pltpu.make_async_copy(s_hbm, sbuf.at[0], load_sem.at[0]), pltpu.make_async_copy(u_hbm, ubuf.at[0], load_sem.at[1])]
     loads += [pltpu.make_async_copy(ints_hbm[n], ints[n], load_sem.at[2 + n]) for n in range(5)]
     for load in loads:
         load.start()
 
     barrier = pltpu.get_barrier_semaphore()
-    heard = jnp.where(is_centre, 31, 1) + jnp.where(is_member, 3, 0) - jnp.where(is_worker, 1, 0)
+    heard = jnp.where(is_centre, 15, 1) + jnp.where(is_member, 3, 0) - jnp.where(is_worker, 1, 0)
     for offset in (-2, -1, 1, 2):
         inside = (place + offset >= 0) & (place + offset < 16)
         heard = heard + jnp.where(inside, 1, 0)
@@ -80,13 +76,17 @@
 
     @pl.when(is_centre)
     def _():
-        @pl.loop(1, 32)
+        @pl.loop(1, 64)
         def _(n):
-            pl.semaphore_signal(barrier, inc=1, device_id={"gy": n // 8, "gz_1": n % 8}, device_id_type=MESH)
-
-        @pl.loop(1, 32)
-        def _(n):
-            pl.semaphore_signal(barrier, inc=1, device_id=replica(n // 8, n % 8), device_id_type=MESH)
+            other = {"gy": (64 - n) // 16, "gz_1": (64 - n) // 2 % 8, "gz_2": (64 - n) % 2}
+            pl.when(n != 63)(lambda: pl.semaphore_signal(barrier, inc=1, device_id=other, device_id_type=MESH))
+
+        pl.semaphore_signal(barrier, inc=1, device_id={"gz_2": 0}, device_id_type=MESH)
+        for n in range(16):
+            other = {"ta": n // 4, "gz_0": n % 4}
+            pl.when(column != n)(
+                functools.partial(pl.semaphore_signal, barrier, inc=1, device_id=other, device_id_type=MESH)
+            )
 
     loads[0].wait()
     loads[1].wait()
@@ -397,52 +397,53 @@
 
     def to_centre():
         return pltpu.make_async_remote_copy(
-            src_ref=mine, dst_ref=slot_b.at[chip], send_sem=send_b, recv_sem=recv_b,
-            device_id={"gy": 0, "gz_1": 0}, device_id_type=MESH,
+            src_ref=mine, dst_ref=slot_b.at[chip * 2 + core], send_sem=send_b, recv_sem=recv_b,
+            device_id={"gy": 0, "gz_1": 0, "gz_2": 1}, device_id_type=MESH,
         )
 
     def to_plane(n):
         return pltpu.make_async_remote_copy(
-            src_ref=sum_b, dst_ref=slot_c.at[x * 8 + r], send_sem=send_c, recv_sem=recv_c,
-            device_id={"ta": n // 8, "gz_0": n % 8 // 2, "gz_2": n % 2}, device_id_type=MESH,
+            src_ref=sum_b, dst_ref=slot_c.at[column], send_sem=send_c, recv_sem=recv_c,
+            device_id={"ta": n // 4, "gz_0": n % 4}, device_id_type=MESH,
         )
 
-    def to_chip(dst):
+    def to_chip(dst, side):
         return pltpu.make_async_remote_copy(
             src_ref=final.at[0], dst_ref=final.at[0], send_sem=send_d, recv_sem=recv_d,
-            device_id={"gy": dst // 8, "gz_1": dst % 8}, device_id_type=MESH,
+            device_id={"gy": dst // 8, "gz_1": dst % 8, "gz_2": side}, device_id_type=MESH,
         )
 
-    outward = (1, 2, 3, 4, 5, 6, 7, 28, 8, 24, 12, 20, 16)
+    outward = [(0, 0)] + [(c, side) for c in (1, 2, 3, 4, 5, 6, 7, 28, 8, 24, 12, 20, 16) for side in (0, 1)]
     is_head = (chip % 4 == 0) & (chip >= 8)
 
     @pl.when(jnp.logical_not(is_centre))
     def _():
         to_centre().start()
-        to_chip(0).wait_recv()
+        to_chip(0, 1).wait_recv()
 
         @pl.when(is_head)
         def _():
             for n in range(1, 4):
-                to_chip(chip + n).start()
+                to_chip(chip + n, core).start()
 
     @pl.when(is_centre)
     def _():
         acc = mine[...]
-        bulk(slot_b.at[pl.ds(1, 31)], recv_b).wait_recv()
-        for n in range(1, 32):
-            acc = acc + slot_b[n]
+        bulk(slot_b.at[pl.ds(0, 63)], recv_b).wait_recv()
+        for n in range(64):
+            if n != 1:
+                acc = acc + slot_b[n]
         sum_b[...] = acc
 
-        for n in range(32):
-            pl.when(x * 8 + r != n)(to_plane(n).start)
-        slot_c[x * 8 + r] = acc
-        bulk(slot_c.at[pl.ds(0, 31)], recv_c).wait_recv()
+        for n in range(16):
+            pl.when(column != n)(to_plane(n).start)
+        slot_c[column] = acc
+        bulk(slot_c.at[pl.ds(0, 15)], recv_c).wait_recv()
         slices = []
         for t in range(4):
-            acc = slot_c[8 * t]
-            for q in range(1, 8):
-                acc = acc + slot_c[8 * t + q]
+            acc = slot_c[4 * t]
+            for q in range(1, 4):
+                acc = acc + slot_c[4 * t + q]
             slices.append(acc)
         quarter = lax.broadcasted_iota(I32, (4, 128), 1) // 32
         for q in range(4):
@@ -453,8 +454,8 @@
             for m in range(3):
                 if m * 4 + q < 9:
                     final[0, m * 4 + q] = rows[m : m + 1, :]
-        for dst in outward:
-            to_chip(dst).start()
+        for dst, side in outward:
+            to_chip(dst, side).start()
 
     for j in range(9):
         out[j : j + 1, :] = final[0, j]
@@ -481,7 +482,7 @@
 
     @pl.when(is_centre)
     def _():
-        bulk(slot_c.at[pl.ds(0, 31)], send_c).wait_send()
+        bulk(slot_c.at[pl.ds(0, 15)], send_c).wait_send()
         bulk(final, send_d).wait_send()
 
 
@@ -512,10 +513,10 @@
             pltpu.VMEM((3, 8, 8, 128), F32),
             pltpu.VMEM((3, 8, 128), I32),
             pltpu.VMEM((4, 128), F32),
-            pltpu.VMEM((32, 4, 128), F32),
+            pltpu.VMEM((64, 4, 128), F32),
             pltpu.VMEM((4, 128), F32),
-            pltpu.VMEM((32, 4, 128), F32),
-            pltpu.VMEM((13, 9, 1, 128), F32),
+            pltpu.VMEM((16, 4, 128), F32),
+            pltpu.VMEM((27, 9, 1, 128), F32),
             pltpu.VMEM((8, 6, 16, 128), jnp.bfloat16),
             pltpu.VMEM((8, 9, 2, 128), jnp.bfloat16),
             pltpu.VMEM((8, 12, 8, 128), F32),

time: 53.8 us -> 53.1 us (0.987)
  Pallas kernels: 52.2 us -> 51.5 us
    pallas_call x1, Pallas kernels: 52.2 us -> 51.5 us  [body(): pl.pallas_call(functools.partial(kernel, nz, scaling), out_shape=jax.Shap...]
where the time goes in v5:
time: 53.1 us; the launch traced here: 52.9 us
  Pallas kernels  51.5 us (97%)
  local copies, waits for them, and re-layouts  1.43 us (3%)
    pallas_call x1, Pallas kernels, body(): pl.pallas_call(functools.partial(kernel, nz, scaling), out_shape=jax.Shap...  51.5 us
    pallas_call x1, local copies, waits for them, and re-layouts, body(): pl.pallas_call(functools.partial(kernel, nz, scaling), out_shape=jax.Shap...  1.43 us

profile of v5, /device:TPU:1, one launch (start us, length us, event | category | flops | bytes accessed | tf_op | source)
XLA Modules:
  0.0 52.9 jit_solution(4450685535595333836)
XLA Ops:
  0.0 51.5 %shard_map.73 = f32[9,128]{1,0:T(8,128)} custom-call(bf16[6,48,128]{2,1,0:T(8,128)(2,1)} %bitcast.9, bf16[9,2,128]{2,1,0:T(2,128)(2,1)} %bitcast.10, s32[4,4]{1,0:T(4,128)} %refs_0_.1, s32[9]{0:T(128)} %refs_1_.1, s32[4]{0:T(128)} %refs_2_.1, s32[4,4]{1,0:T(4,128)} %refs_3_.1, s32[4,4]{1,0:T(4,128)} %refs_4_.1), custom_call_target="tpu_custom_call" | custom-call | tf_op jit(solution)/shard_map/pallas_call | solution.py:497
  51.5 1.4 %copy.9 = f32[9,128]{0,1:T(8,128)} copy(f32[9,128]{1,0:T(8,128)} %shard_map.73) | data formatting | bytes 9216 | tf_op jit(solution)/shard_map/pallas_call | solution.py:497

commit v6 on v5

--- a/solution.py
+++ b/solution.py
@@ -59,7 +59,17 @@
         load.start()
 
     barrier = pltpu.get_barrier_semaphore()
-    heard = jnp.where(is_centre, 15, 1) + jnp.where(is_member, 3, 0) - jnp.where(is_worker, 1, 0)
+    @pl.when(is_worker)
+    def _():
+        row_w = gy0 + jnp.where(at_end, 3, 0)
+        for n in range(4):
+            other = seat(row_w + jnp.where(at_end, 1, 0), jnp.where(at_end, n, 12 + n))
+            pl.semaphore_signal(barrier, inc=1, device_id=other, device_id_type=MESH)
+        for n in range(4):
+            other = seat(row_w + jnp.where(at_end, 0, 1), jnp.where(at_end, 12 + n, n))
+            pl.semaphore_signal(barrier, inc=1, device_id=other, device_id_type=MESH)
+
+    heard = jnp.where(is_centre, 15, 1) + jnp.where(is_member, 3, 0)
     for offset in (-2, -1, 1, 2):
         inside = (place + offset >= 0) & (place + offset < 16)
         heard = heard + jnp.where(inside, 1, 0)
@@ -67,12 +77,6 @@
         @pl.when(inside)
         def _():
             pl.semaphore_signal(barrier, inc=1, device_id=along(offset), device_id_type=MESH)
-
-    for n in range(8):
-        @pl.when(is_worker & (n != member))
-        def _():
-            other = seat(row_a, 12 + n) if n < 4 else seat(row_a + 1, n - 4)
-            pl.semaphore_signal(barrier, inc=1, device_id=other, device_id_type=MESH)
 
     @pl.when(is_centre)
     def _():
@@ -105,9 +109,6 @@
     offsets = (-2, -1, 2, -1, 1, 2)
     goes = [(place + o >= 0) & (place + o < 16) for o in offsets]
     comes = [(place - o >= 0) & (place - o < 16) for o in offsets]
-    for n in (3, 4, 5, 1, 0, 2):
-        pl.when(goes[n])(halo[n].start)
-
     def bulk(ref, sem):
         return pltpu.make_async_remote_copy(
             src_ref=ref, dst_ref=ref, send_sem=sem, recv_sem=sem, device_id={"gy": (hi + 1) % 4}, device_id_type=MESH
@@ -115,21 +116,21 @@
 
     def to_worker(n):
         third, spot = n % 3, first + n % 3
-        row = row_a + jnp.where(at_end, 0, 1)
+        row = row_a + jnp.where(at_end, 1, 0)
         src = sbuf.at[0, :, pl.ds(third * 16, 16), :] if n < 3 else ubuf.at[0]
         dst, sem = (xbuf, recv_x) if n < 3 else (xlink, recv_l)
         side = jnp.where(place >= 12, 0, 1)
-        near = pltpu.make_async_copy(src, dst.at[member], sem.at[side])
-        far = pltpu.make_async_remote_copy(
+        return pltpu.make_async_remote_copy(
             src_ref=src, dst_ref=dst.at[member], send_sem=send_x.at[n // 3], recv_sem=sem.at[side],
             device_id=seat(row, spot), device_id_type=MESH,
         )
-        return near, far, is_member & (place == spot), is_member & (place != spot)
-
-    for n in (3, 4, 5, 0, 1, 2):
-        near, far, here, there = to_worker(n)
-        pl.when(here)(near.start)
-        pl.when(there)(far.start)
+    @pl.when(is_member)
+    def _():
+        for n in (3, 4, 5, 0, 1, 2):
+            to_worker(n).start()
+
+    for n in (3, 4, 5, 1, 0, 2):
+        pl.when(goes[n])(halo[n].start)
 
     for load in loads[2:]:
         load.wait()
@@ -152,7 +153,7 @@
     for p in range(4):
         mom = jnp.where(p_id == p, momenta[p], mom)
         src = jnp.where(p_id == p, source_z[x, p], src)
-    corner = jnp.where(at_end, 12 - place, -4 - place)
+    corner = jnp.where(at_end, -4 - place, 12 - place)
     for n in range(5):
         turns = (mom * (corner + n if n < 4 else -2)) & (nz - 1)
         angle = turns.astype(F32) * (2.0 * math.pi / nz)
@@ -462,12 +463,7 @@
 
     for n in range(6):
         pl.when(goes[n])(halo[n].wait_send)
-    @pl.when(is_member & is_worker)
-    def _():
-        bulk(sbuf.at[0, :, pl.ds(0, 32), :], send_x.at[0]).wait_send()
-        bulk(ubuf.at[pl.ds(0, 2)], send_x.at[1]).wait_send()
-
-    @pl.when(is_member & jnp.logical_not(is_worker))
+    @pl.when(is_member)
     def _():
         bulk(sbuf.at[0], send_x.at[0]).wait_send()
         bulk(ubuf.at[pl.ds(0, 3)], send_x.at[1]).wait_send()

time: 53.1 us -> 51.3 us (0.966)
  Pallas kernels: 51.5 us -> 49.6 us
    pallas_call x1, Pallas kernels: 51.5 us -> 49.6 us  [body(): pl.pallas_call(functools.partial(kernel, nz, scaling), out_shape=jax.Shap...]
where the time goes in v6:
time: 51.3 us; the launch traced here: 51 us
  Pallas kernels  49.6 us (97%)
  local copies, waits for them, and re-layouts  1.43 us (3%)
    pallas_call x1, Pallas kernels, body(): pl.pallas_call(functools.partial(kernel, nz, scaling), out_shape=jax.Shap...  49.6 us
    pallas_call x1, local copies, waits for them, and re-layouts, body(): pl.pallas_call(functools.partial(kernel, nz, scaling), out_shape=jax.Shap...  1.43 us

profile of v6, /device:TPU:1, one launch (start us, length us, event | category | flops | bytes accessed | tf_op | source)
XLA Modules:
  0.0 51.0 jit_solution(4511619687091425652)
XLA Ops:
  0.0 49.6 %shard_map.73 = f32[9,128]{1,0:T(8,128)} custom-call(bf16[6,48,128]{2,1,0:T(8,128)(2,1)} %bitcast.9, bf16[9,2,128]{2,1,0:T(2,128)(2,1)} %bitcast.10, s32[4,4]{1,0:T(4,128)} %refs_0_.1, s32[9]{0:T(128)} %refs_1_.1, s32[4]{0:T(128)} %refs_2_.1, s32[4,4]{1,0:T(4,128)} %refs_3_.1, s32[4,4]{1,0:T(4,128)} %refs_4_.1), custom_call_target="tpu_custom_call" | custom-call | tf_op jit(solution)/shard_map/pallas_call | solution.py:493
  49.6 1.4 %copy.9 = f32[9,128]{0,1:T(8,128)} copy(f32[9,128]{1,0:T(8,128)} %shard_map.73) | data formatting | bytes 9216 | tf_op jit(solution)/shard_map/pallas_call | solution.py:493

commit v7 on v6

--- a/solution.py
+++ b/solution.py
@@ -316,31 +316,39 @@
         halo[0].wait_recv()
         bring(2, 1)
 
-    @pl.when(comes[2])
-    def _():
-        keep(wil, 2, product(link(ubuf, 3), link(ubuf, 2)), dagger=True)
-        halo[2].wait_recv()
-        bring(3, 2)
-
-    for line, n in ((0, 1), (1, 0), (2, 2)):
+    for line, n in ((0, 1), (1, 0)):
         @pl.when(jnp.logical_not(comes[n]))
         def _():
             clear(line)
 
-    def moved_pairs(rr, n, acc):
+    def ahead_pairs(rr, n, acc):
         acc = list(acc)
         for a in range(3):
             re_at, im_at = n + 6 * a, 18 + n + 6 * a
             here = (left[rr, re_at], left[rr, im_at])
+            mac(acc, 0, here, (fields[0, re_at], fields[0, im_at]))
+            mac(acc, 1, here, (fields[1, re_at], fields[1, im_at]))
+        return tuple(acc)
+
+    def behind_pairs(rr, n, acc):
+        acc = list(acc)
+        for a in range(3):
+            re_at, im_at = n + 6 * a, 18 + n + 6 * a
             behind = (roll4(fields[2, re_at], rr), roll4(fields[2, im_at], rr))
-            one, two = (fields[0, re_at], fields[0, im_at]), (fields[1, re_at], fields[1, im_at])
-            mac(acc, 0, here, one)
-            mac(acc, 1, here, two)
-            mac(acc, 2, behind, one)
-            mac(acc, 3, behind, two)
+            mac(acc, 0, behind, (fields[0, re_at], fields[0, im_at]))
+            mac(acc, 1, behind, (fields[1, re_at], fields[1, im_at]))
         return tuple(acc)
 
-    regular((1, 2, 3, 4), moved_pairs, ((1, 2), (3, 4)), total)
+    regular((1, 2), ahead_pairs, ((1, 2), ()), total)
+
+    @pl.when(comes[2])
+    def _():
+        keep(wil, 2, product(link(ubuf, 3), link(ubuf, 2)), dagger=True)
+        halo[2].wait_recv()
+        bring(3, 2)
+
+    pl.when(jnp.logical_not(comes[2]))(lambda: clear(2))
+    regular((3, 4), behind_pairs, ((), (3, 4)), total)
     mine[...] = turned(total[0], None) + turned(total[1], 4)
 
     @pl.when(is_worker)
@@ -414,18 +422,19 @@
             device_id={"gy": dst // 8, "gz_1": dst % 8, "gz_2": side}, device_id_type=MESH,
         )
 
-    outward = [(0, 0)] + [(c, side) for c in (1, 2, 3, 4, 5, 6, 7, 28, 8, 24, 12, 20, 16) for side in (0, 1)]
-    is_head = (chip % 4 == 0) & (chip >= 8)
+    outward = [(0, 0)] + [(c, side) for c in (1, 2, 3, 4, 24, 8, 16) for side in (0, 1)]
+    heads = [(chip == 4, 4), ((chip == 8) | (chip == 16) | (chip == 24), 8)]
 
     @pl.when(jnp.logical_not(is_centre))
     def _():
         to_centre().start()
         to_chip(0, 1).wait_recv()
 
-        @pl.when(is_head)
-        def _():
-            for n in range(1, 4):
-                to_chip(chip + n, core).start()
+        for is_head, end in heads:
+            @pl.when(is_head)
+            def _():
+                for n in range(1, end):
+                    to_chip(chip + n, core).start()
 
     @pl.when(is_centre)
     def _():
@@ -472,9 +481,10 @@
     def _():
         to_centre().wait_send()
 
-        @pl.when(is_head)
-        def _():
-            bulk(final.at[pl.ds(0, 3)], send_d).wait_send()
+        for is_head, end in heads:
+            @pl.when(is_head)
+            def _():
+                bulk(final.at[pl.ds(0, end - 1)], send_d).wait_send()
 
     @pl.when(is_centre)
     def _():
@@ -512,7 +522,7 @@
             pltpu.VMEM((64, 4, 128), F32),
             pltpu.VMEM((4, 128), F32),
             pltpu.VMEM((16, 4, 128), F32),
-            pltpu.VMEM((27, 9, 1, 128), F32),
+            pltpu.VMEM((15, 9, 1, 128), F32),
             pltpu.VMEM((8, 6, 16, 128), jnp.bfloat16),
             pltpu.VMEM((8, 9, 2, 128), jnp.bfloat16),
             pltpu.VMEM((8, 12, 8, 128), F32),

time: 51.3 us -> 50.8 us (level)
  no operation moved by 1% of the time
where the time goes in v7:
time: 50.8 us; the launch traced here: 50.6 us
  Pallas kernels  49.2 us (97%)
  local copies, waits for them, and re-layouts  1.43 us (3%)
    pallas_call x1, Pallas kernels, body(): pl.pallas_call(functools.partial(kernel, nz, scaling), out_shape=jax.Shap...  49.2 us
    pallas_call x1, local copies, waits for them, and re-layouts, body(): pl.pallas_call(functools.partial(kernel, nz, scaling), out_shape=jax.Shap...  1.43 us

profile of v7, /device:TPU:1, one launch (start us, length us, event | category | flops | bytes accessed | tf_op | source)
XLA Modules:
  0.0 50.6 jit_solution(2759561366730648253)
XLA Ops:
  0.0 49.2 %shard_map.73 = f32[9,128]{1,0:T(8,128)} custom-call(bf16[6,48,128]{2,1,0:T(8,128)(2,1)} %bitcast.9, bf16[9,2,128]{2,1,0:T(2,128)(2,1)} %bitcast.10, s32[4,4]{1,0:T(4,128)} %refs_0_.1, s32[9]{0:T(128)} %refs_1_.1, s32[4]{0:T(128)} %refs_2_.1, s32[4,4]{1,0:T(4,128)} %refs_3_.1, s32[4,4]{1,0:T(4,128)} %refs_4_.1), custom_call_target="tpu_custom_call" | custom-call | tf_op jit(solution)/shard_map/pallas_call | solution.py:503
  49.2 1.4 %copy.9 = f32[9,128]{0,1:T(8,128)} copy(f32[9,128]{1,0:T(8,128)} %shard_map.73) | data formatting | bytes 9216 | tf_op jit(solution)/shard_map/pallas_call | solution.py:503

commit v8 on v7

--- a/solution.py
+++ b/solution.py
@@ -43,8 +43,8 @@
     is_member = (place >= 12) | (place < 4)
     member = jnp.where(place >= 12, place - 12, place + 4)
     row_a = jnp.where(place >= 12, gy0, (gy0 + 3) % 4)
-    is_worker = jnp.where(at_end, place >= 13, place < 3)
-    first = jnp.where(at_end, 13, 0)
+    first = jnp.where(at_end, 6, 0)
+    is_worker = (place >= first) & (place < first + 3)
 
     def seat(row, spot):
         return {"gz_0": row % 4, "gz_1": spot // 2, "gz_2": spot % 2}

time: 50.8 us -> 49.9 us (0.982)
  Pallas kernels: 49.2 us -> 48.2 us
    pallas_call x1, Pallas kernels: 49.2 us -> 48.2 us  [body(): pl.pallas_call(functools.partial(kernel, nz, scaling), out_shape=jax.Shap...]
where the time goes in v8:
time: 49.9 us; the launch traced here: 49.7 us
  Pallas kernels  48.2 us (97%)
  local copies, waits for them, and re-layouts  1.43 us (3%)
    pallas_call x1, Pallas kernels, body(): pl.pallas_call(functools.partial(kernel, nz, scaling), out_shape=jax.Shap...  48.2 us
    pallas_call x1, local copies, waits for them, and re-layouts, body(): pl.pallas_call(functools.partial(kernel, nz, scaling), out_shape=jax.Shap...  1.43 us

profile of v8, /device:TPU:1, one launch (start us, length us, event | category | flops | bytes accessed | tf_op | source)
XLA Modules:
  0.0 49.7 jit_solution(3685605352383514874)
XLA Ops:
  0.0 48.2 %shard_map.73 = f32[9,128]{1,0:T(8,128)} custom-call(bf16[6,48,128]{2,1,0:T(8,128)(2,1)} %bitcast.9, bf16[9,2,128]{2,1,0:T(2,128)(2,1)} %bitcast.10, s32[4,4]{1,0:T(4,128)} %refs_0_.1, s32[9]{0:T(128)} %refs_1_.1, s32[4]{0:T(128)} %refs_2_.1, s32[4,4]{1,0:T(4,128)} %refs_3_.1, s32[4,4]{1,0:T(4,128)} %refs_4_.1), custom_call_target="tpu_custom_call" | custom-call | tf_op jit(solution)/shard_map/pallas_call | solution.py:503
  48.2 1.4 %copy.9 = f32[9,128]{0,1:T(8,128)} copy(f32[9,128]{1,0:T(8,128)} %shard_map.73) | data formatting | bytes 9216 | tf_op jit(solution)/shard_map/pallas_call | solution.py:503

commit v9 on v8

--- a/solution.py
+++ b/solution.py
@@ -43,7 +43,7 @@
     is_member = (place >= 12) | (place < 4)
     member = jnp.where(place >= 12, place - 12, place + 4)
     row_a = jnp.where(place >= 12, gy0, (gy0 + 3) % 4)
-    first = jnp.where(at_end, 6, 0)
+    first = jnp.where(at_end, 7, 0)
     is_worker = (place >= first) & (place < first + 3)
 
     def seat(row, spot):

time: 49.9 us -> 49.5 us (level)
  no operation moved by 1% of the time
where the time goes in v9:
time: 49.5 us; the launch traced here: 49.3 us
  Pallas kernels  47.8 us (97%)
  local copies, waits for them, and re-layouts  1.43 us (3%)
    pallas_call x1, Pallas kernels, body(): pl.pallas_call(functools.partial(kernel, nz, scaling), out_shape=jax.Shap...  47.8 us
    pallas_call x1, local copies, waits for them, and re-layouts, body(): pl.pallas_call(functools.partial(kernel, nz, scaling), out_shape=jax.Shap...  1.43 us

profile of v9, /device:TPU:1, one launch (start us, length us, event | category | flops | bytes accessed | tf_op | source)
XLA Modules:
  0.0 49.3 jit_solution(7357715950888578078)
XLA Ops:
  0.0 47.8 %shard_map.73 = f32[9,128]{1,0:T(8,128)} custom-call(bf16[6,48,128]{2,1,0:T(8,128)(2,1)} %bitcast.9, bf16[9,2,128]{2,1,0:T(2,128)(2,1)} %bitcast.10, s32[4,4]{1,0:T(4,128)} %refs_0_.1, s32[9]{0:T(128)} %refs_1_.1, s32[4]{0:T(128)} %refs_2_.1, s32[4,4]{1,0:T(4,128)} %refs_3_.1, s32[4,4]{1,0:T(4,128)} %refs_4_.1), custom_call_target="tpu_custom_call" | custom-call | tf_op jit(solution)/shard_map/pallas_call | solution.py:503
  47.8 1.4 %copy.9 = f32[9,128]{0,1:T(8,128)} copy(f32[9,128]{1,0:T(8,128)} %shard_map.73) | data formatting | bytes 9216 | tf_op jit(solution)/shard_map/pallas_call | solution.py:503
